TPU v7x, 32 devices: a whole 2x2x4 slice. The times are simulated.
32 devices in a mesh: groups: 2 (over x), replica: 16 (over z, y, core).
Axes of the slice: x: 2, y: 2, z: 4, core: 2. Of those that a mesh axis runs over, the one named last changes fastest.
Arguments:
- tokens: bfloat16 [32768, 2048], P(('groups', 'replica')), parts along dimension 0, may hold values from -6 to 6
- pseudo_keys: bfloat16 [32, 2048, 512], P(('groups', 'replica')), parts along dimension 0, may hold values from -0.875 to 0.875
- pseudo_values: bfloat16 [32, 2048, 512], P(('groups', 'replica')), parts along dimension 0, may hold values from -0.875 to 0.875
- master_keys: float32 [4096, 512], P(('groups', 'replica')), parts along dimension 0, may hold values from -0.125 to 0.125
- moment_keys: float32 [4096, 512], P(('groups', 'replica')), parts along dimension 0, may hold values from -0.125 to 0.125
- master_values: float32 [4096, 512], P(('groups', 'replica')), parts along dimension 0, may hold values from -0.125 to 0.125
- moment_values: float32 [4096, 512], P(('groups', 'replica')), parts along dimension 0, may hold values from -0.125 to 0.125
- outer_hyper: float32 [4], P('groups'), parts along dimension 0, may hold values from 0.5 to 0.95
Outputs:
- eval_keys: bfloat16 [32768, 512], P(('groups', 'replica')), parts along dimension 0
- eval_values: bfloat16 [32768, 512], P(('groups', 'replica')), parts along dimension 0
- new_master_keys: float32 [4096, 512], P(('groups', 'replica')), parts along dimension 0
- new_moment_keys: float32 [4096, 512], P(('groups', 'replica')), parts along dimension 0
- new_master_values: float32 [4096, 512], P(('groups', 'replica')), parts along dimension 0
- new_moment_values: float32 [4096, 512], P(('groups', 'replica')), parts along dimension 0
There are 2 independent parts, one for each index of `groups`. A program takes and returns all parts, laid end to end along the dimension named above; each array names one. Nothing has to cross between parts.
All inputs are finite; a program needn't handle non-finite values.
Results may differ from a plain program's by a relative error of at most 0.0049.
Values may be sent and summed in bfloat16 or wider, within the bound.
No kernel may reach another device: no remote copies, remote signals or barrier semaphores. Data moves between devices by JAX's collectives and lax.ppermute only.
A program may use at most 128 MiB of HBM per device.

v0:
```python
import functools

import jax
import jax.numpy as jnp
from jax import lax
from jax.experimental import pallas as pl
from jax.experimental.pallas import tpu as pltpu
from jax.sharding import PartitionSpec as P


BF16, F32 = jnp.bfloat16, jnp.float32
IN_VMEM = pl.BlockSpec(memory_space=pltpu.VMEM)
IN_HBM = pl.BlockSpec(memory_space=pltpu.HBM)


def swap(array, stride):
    replicas = lax.axis_size("replica")
    return lax.ppermute(array, "replica", [(r, r ^ stride) for r in range(replicas)])


def call(kernel, arrays, out, *, specs=None, scratch=(), hold=True, flops=10**6, **options):
    if specs is None:
        specs = [IN_VMEM] * len(arrays)
    holders = {id(IN_VMEM): pltpu.VMEM, id(IN_HBM): pltpu.HBM}
    arrays = [
        pltpu.with_memory_space_constraint(a, holders[id(spec)]) if id(spec) in holders else a
        for a, spec in zip(arrays, specs)
    ]
    shape = pltpu.VMEM if hold else jax.ShapeDtypeStruct
    return pl.pallas_call(
        kernel,
        out_shape=[shape(*o) for o in out],
        in_specs=specs,
        out_specs=[IN_VMEM] * len(out),
        scratch_shapes=scratch,
        cost_estimate=pl.CostEstimate(flops=flops, bytes_accessed=10**6, transcendentals=0),
        compiler_params=pltpu.CompilerParams(vmem_limit_bytes=8 * 2**20),
        **options,
    )(*arrays)


def copy_kernel(plan, blocks, *refs):
    *outs, sem = refs
    me = lax.axis_index("replica")
    copies = [
        pltpu.make_async_copy(blocks.at[me ^ block], outs[o].at[place], sem.at[n])
        for n, (block, o, place) in enumerate(plan)
    ]
    for copy in copies:
        copy.start()
    for copy in copies:
        copy.wait()


def add_kernel(terms, outs, *refs):
    for o, rows in enumerate(terms):
        out = refs[outs + o]
        for place, parts in enumerate(rows):
            total = None
            for ref, at in parts:
                part = refs[ref][at].astype(F32)
                total = part if total is None else total + part
            out[place] = total.astype(out.dtype)


def nesterov(summed, master, moment, hyper, replicas):
    outer_rate, outer_mom = hyper[:, 0:1], hyper[:, 1:2]
    averaged = summed / replicas
    moment_new = outer_mom * moment + averaged
    master_new = master - outer_rate * (averaged + outer_mom * moment_new)
    return master_new, moment_new


def weights_kernel(replicas, places, hyper, master, moment, *refs):
    *parts, weights, summed = refs
    total = parts[0][places[0]].astype(F32)
    for part, at in zip(parts[1:], places[1:]):
        total = total + part[at].astype(F32)
    summed[...] = total
    master_new, _ = nesterov(total, master[...], moment[...], hyper, replicas)
    weights[0] = master_new.astype(BF16)


def state_kernel(replicas, hyper, master, moment, summed, master_out, moment_out):
    master_new, moment_new = nesterov(
        summed[...], master[...], moment[...], hyper, replicas
    )
    master_out[...] = master_new
    moment_out[...] = moment_new


def product_kernel(height, blocks, groups, tokens, *refs):
    slabs, out = refs[:groups], refs[-1]
    weights = jnp.concatenate([s[...].reshape(-1, s.shape[-1]) for s in slabs], axis=0)
    rows = jnp.concatenate([tokens[:, k * height : (k + 1) * height] for k in blocks], axis=1)
    total = jnp.dot(rows, weights, preferred_element_type=F32)
    if len(refs) > groups + 1:
        total = total + refs[groups][...]
    out[...] = total.astype(out.dtype)


def columns_kernel(rows, tokens, out, sem):
    me = lax.axis_index("replica")
    copies = [
        pltpu.make_async_copy(
            tokens.at[:, pl.ds(pl.multiple_of((me ^ block) * rows, rows), rows)],
            out.at[:, pl.ds(block * rows, rows)],
            sem.at[block],
        )
        for block in range(tokens.shape[1] // rows)
    ]
    for copy in copies:
        copy.start()
    for copy in copies:
        copy.wait()


SUMS = {
    "k": [(4, [4, 6, 12, 14]), (2, [2, 10]), (8, [8])],
    "v": [(2, [2]), (2, [10, 14]), (2, [6]), (4, [4]), (4, [12]), (8, [8])],
}
GATHERS = {
    "k": [(2, [2]), (4, [4]), (8, [8]), (4, [6, 12]), (2, [10]), (4, [14])],
    "v": [(4, [4]), (2, [2]), (8, [8]), (2, [6, 10]), (4, [12]), (2, [14])],
}


def plain_sums(depth):
    half = depth // 2
    far = [4 * j for j in range(half, depth)]
    near = [4 * j for j in range(half)]
    over = [(2, [b + 2 for b in part]) for part in (far, near)]
    return over + [(b, [b]) for b in far + near[1:]]


def plain_gathers(depth):
    return [(stride, blocks) for stride, blocks in reversed(plain_sums(depth))]


def steps_of(groups):
    steps, step, count = [], [], 0
    for n, (blocks, _) in enumerate(groups[:-1]):
        step += [(n, 0), (n, 1)]
        count += 2 * len(blocks)
        if count >= 4:
            steps.append(step)
            step, count = [], 0
    last = len(groups) - 1
    return steps + ([step] if step else []) + [[(last, 0)], [(last, 1)]]


def body(
    tokens,
    pseudo_keys,
    pseudo_values,
    master_keys,
    moment_keys,
    master_values,
    moment_values,
    outer_hyper,
):
    replicas = lax.axis_size("replica")
    rows, width = master_keys.shape
    depth = replicas // 4
    me = lax.axis_index("replica")
    slab = (rows, width)
    hyper = outer_hyper.reshape(1, -1)

    def add(rows_of, dtype):
        arrays = []
        for array, _ in [term for row in rows_of for term in row]:
            if not any(array is other for other in arrays):
                arrays.append(array)
        index = {id(array): n for n, array in enumerate(arrays)}
        terms = [[[(index[id(array)], at) for array, at in row] for row in rows_of]]
        (total,) = call(
            functools.partial(add_kernel, terms, len(arrays)),
            arrays,
            [((len(rows_of), *slab), dtype)],
        )
        return total

    def pieces(pseudo, blocks):
        plan = [(b + side, o, n) for o, side in enumerate((1, 0)) for n, b in enumerate(blocks)]
        return call(
            functools.partial(copy_kernel, plan),
            [pseudo[0].reshape(replicas, *slab)],
            [((len(blocks), *slab), BF16)] * 2,
            specs=[IN_HBM],
            scratch=[pltpu.SemaphoreType.DMA((len(plan),))],
        )

    def reduce(pseudo, transfers):
        order = [b for _, blocks in transfers for b in blocks] + [0]
        terms = {}
        for part in (order[:depth], order[depth:]):
            partner, own = pieces(pseudo, part)
            partner = swap(partner, 1)
            terms.update({b: [(own, n), (partner, n)] for n, b in enumerate(part)})
        for stride, blocks in transfers:
            sent = add([terms[b] for b in blocks], BF16)
            got = swap(sent, stride)
            for n, b in enumerate(blocks):
                terms[b ^ stride].append((got, n))
        return terms[0]

    def weigh(terms, master, moment):
        weights, summed = call(
            functools.partial(weights_kernel, replicas, [at for _, at in terms]),
            [hyper, master, moment, *[array for array, _ in terms]],
            [((1, *slab), BF16), (slab, F32)],
        )
        state = call(
            functools.partial(state_kernel, replicas),
            [hyper, master, moment, summed],
            [(slab, F32)] * 2,
            hold=False,
        )
        return weights, state

    def gather(weights, transfers):
        groups = [([0], weights)]
        for stride, blocks in transfers:
            parents = [b ^ stride for b in blocks]
            held = [array for group, array in groups if group == parents]
            if not held:
                rows_of = [
                    [(array, group.index(b))]
                    for b in parents
                    for group, array in groups
                    if b in group
                ]
                held = [add(rows_of, BF16)]
            groups.append((list(blocks), swap(held[0], stride)))
        pairs = [swap(array, 1) for _, array in groups]
        return groups, pairs

    if rows % 128 == 0:
        (columns,) = call(
            functools.partial(columns_kernel, rows),
            [tokens],
            [(tokens.shape, BF16)],
            specs=[IN_HBM],
            scratch=[pltpu.SemaphoreType.DMA((replicas,))],
        )

    def project(groups, pairs):
        arrivals = [
            [(blocks, array), ([b + 1 for b in blocks], pair)]
            for (blocks, array), pair in zip(groups, pairs)
        ]
        if rows % 128:
            whole = jnp.zeros((replicas, *slab), BF16)
            for blocks, array in [a for both in arrivals for a in both]:
                whole = whole.at[me ^ jnp.array(blocks)].set(array)
            return jnp.dot(tokens, whole.reshape(-1, width), preferred_element_type=F32).astype(BF16)
        total = None
        steps = steps_of(groups)
        for i, step in enumerate(steps):
            last = i == len(steps) - 1
            taken = [arrivals[n][side] for n, side in step]
            blocks = [b for part, _ in taken for b in part]
            arrays = [columns] + [array for _, array in taken] + ([] if total is None else [total])
            (total,) = call(
                functools.partial(product_kernel, rows, blocks, len(step)),
                arrays,
                [((tokens.shape[0], width), BF16 if last else F32)],
                flops=2 * tokens.shape[0] * len(blocks) * rows * width,
                hold=not last,
            )
        return total

    def stream(pseudo, master, moment, s):
        sums = SUMS[s] if depth == 4 else plain_sums(depth)
        gathers = GATHERS[s] if depth == 4 else plain_gathers(depth)
        weights, state = weigh(reduce(pseudo, sums), master, moment)
        return project(*gather(weights, gathers)), state

    projected_keys, state_k = stream(pseudo_keys, master_keys, moment_keys, "k")
    projected_values, state_v = stream(pseudo_values, master_values, moment_values, "v")
    return (projected_keys, projected_values, *state_k, *state_v)


def solution(mesh):
    spec = P(("groups", "replica"), None)
    stacked = P(("groups", "replica"), None, None)
    in_specs = (spec, stacked, stacked, spec, spec, spec, spec, P("groups"))
    out_specs = (spec,) * 6

    return jax.shard_map(body, mesh=mesh, in_specs=in_specs, out_specs=out_specs, check_vma=False)
```

profile of v0, /device:TPU:0, one launch (start us, length us, event | category | flops | bytes accessed | tf_op | source)
XLA Modules:
  0.0 81.5 jit_solution(13206129037375091977)
XLA Ops:
  0.6 1.4 %shard_map.129 = (bf16[4,128,512]{2,1,0:T(8,128)(2,1)S(1)}, bf16[4,128,512]{2,1,0:T(8,128)(2,1)S(1)}) custom-call(bf16[16,128,512]{2,1,0:T(8,128)(2,1)} %bitcast.9), custom_call_target="tpu_custom_call" | custom-call | flops 1000000 | bytes 1000000 | tf_op jit(solution)/shard_map/pallas_call | solution.py:30
  2.0 0.6 collective-permute-start.1
  2.6 1.3 %shard_map.142 = (bf16[4,128,512]{2,1,0:T(8,128)(2,1)S(1)}, bf16[4,128,512]{2,1,0:T(8,128)(2,1)S(1)}) custom-call(bf16[16,128,512]{2,1,0:T(8,128)(2,1)} %bitcast.7), custom_call_target="tpu_custom_call" | custom-call | flops 1000000 | bytes 1000000 | tf_op jit(solution)/shard_map/pallas_call | solution.py:30
  4.0 1.3 %shard_map.141 = (bf16[4,128,512]{2,1,0:T(8,128)(2,1)S(1)}, bf16[4,128,512]{2,1,0:T(8,128)(2,1)S(1)}) custom-call(bf16[16,128,512]{2,1,0:T(8,128)(2,1)} %bitcast.8), custom_call_target="tpu_custom_call" | custom-call | flops 1000000 | bytes 1000000 | tf_op jit(solution)/shard_map/pallas_call | solution.py:30
  5.4 0.6 collective-permute-start.18
  5.9 1.3 %shard_map.128 = (bf16[4,128,512]{2,1,0:T(8,128)(2,1)S(1)}, bf16[4,128,512]{2,1,0:T(8,128)(2,1)S(1)}) custom-call(bf16[16,128,512]{2,1,0:T(8,128)(2,1)} %bitcast.10), custom_call_target="tpu_custom_call" | custom-call | flops 1000000 | bytes 1000000 | tf_op jit(solution)/shard_map/pallas_call | solution.py:30
  7.5 3.1 %collective-permute-start.2 = (bf16[4,128,512]{2,1,0:T(8,128)(2,1)S(1)}, bf16[4,128,512]{2,1,0:T(8,128)(2,1)S(1)}, u32[]{:S(2)}, u32[]{:S(2)}) collective-permute-start(bf16[4,128,512]{2,1,0:T(8,128)(2,1)S(1)} %shard_map.130), channel_id=1, source_target_pairs={{0,4},{1,5},{2,6},{3,7},{4,0},{5,1},{6,2},{7,3},{8,12},{9,13},{10,... | collective-permute-start | bytes 1572872 | tf_op jit(solution)/shard_map/ppermute | solution.py:18
  10.7 1.6 %collective-permute-start.23 = (bf16[2,128,512]{2,1,0:T(8,128)(2,1)S(1)}, bf16[2,128,512]{2,1,0:T(8,128)(2,1)S(1)}, u32[]{:S(2)}, u32[]{:S(2)}) collective-permute-start(bf16[2,128,512]{2,1,0:T(8,128)(2,1)S(1)} %shard_map.146), channel_id=1, source_target_pairs={{0,2},{1,3},{2,0},{3,1},{4,6},{5,7},{6,4},{7,5},{8,10},{9,11},{10,... | collective-permute-start | bytes 786440 | tf_op jit(solution)/shard_map/ppermute | solution.py:18
  12.3 0.6 collective-permute-start.21
  12.9 7.0 %collective-permute-done.23.refs_2_ = bf16[2,128,512]{2,1,0:T(8,128)(2,1)S(1)} collective-permute-done((bf16[2,128,512]{2,1,0:T(8,128)(2,1)S(1)}, bf16[2,128,512]{2,1,0:T(8,128)(2,1)S(1)}, u32[]{:S(2)}, u32[]{:S(2)}) %collective-permute-start.23) | collective-permute-done | bytes 262176 | tf_op jit(solution)/shard_map/ppermute | solution.py:18
  20.1 3.3 %collective-permute-done.2.refs_2_ = bf16[4,128,512]{2,1,0:T(8,128)(2,1)S(1)} collective-permute-done((bf16[4,128,512]{2,1,0:T(8,128)(2,1)S(1)}, bf16[4,128,512]{2,1,0:T(8,128)(2,1)S(1)}, u32[]{:S(2)}, u32[]{:S(2)}) %collective-permute-start.2) | collective-permute-done | bytes 524320 | tf_op jit(solution)/shard_map/ppermute | solution.py:18
  23.5 2.0 %collective-permute-start.3 = (bf16[2,128,512]{2,1,0:T(8,128)(2,1)S(1)}, bf16[2,128,512]{2,1,0:T(8,128)(2,1)S(1)}, u32[]{:S(2)}, u32[]{:S(2)}) collective-permute-start(bf16[2,128,512]{2,1,0:T(8,128)(2,1)S(1)} %shard_map.131), channel_id=1, source_target_pairs={{0,2},{1,3},{2,0},{3,1},{4,6},{5,7},{6,4},{7,5},{8,10},{9,11},{10,... | collective-permute-start | bytes 786440 | tf_op jit(solution)/shard_map/ppermute | solution.py:18
  25.8 2.1 %collective-permute-start.22 = (bf16[1,128,512]{2,1,0:T(8,128)(2,1)S(1)}, bf16[1,128,512]{2,1,0:T(8,128)(2,1)S(1)}, u32[]{:S(2)}, u32[]{:S(2)}) collective-permute-start(bf16[1,128,512]{2,1,0:T(8,128)(2,1)S(1)} %shard_map.145), channel_id=1, source_target_pairs={{0,4},{1,5},{2,6},{3,7},{4,0},{5,1},{6,2},{7,3},{8,12},{9,13},{10,... | collective-permute-start | bytes 393224 | tf_op jit(solution)/shard_map/ppermute | solution.py:18
  28.0 2.7 %collective-permute-start.25 = (bf16[1,128,512]{2,1,0:T(8,128)(2,1)S(1)}, bf16[1,128,512]{2,1,0:T(8,128)(2,1)S(1)}, u32[]{:S(2)}, u32[]{:S(2)}) collective-permute-start(bf16[1,128,512]{2,1,0:T(8,128)(2,1)S(1)} %shard_map.148), channel_id=1, source_target_pairs={{0,8},{1,9},{2,10},{3,11},{4,12},{5,13},{6,14},{7,15},{8,0},{9,1},... | collective-permute-start | bytes 393224 | tf_op jit(solution)/shard_map/ppermute | solution.py:18
  30.6 2.8 %collective-permute-done.20.refs_2_ = bf16[1,128,512]{2,1,0:T(8,128)(2,1)S(1)} collective-permute-done((bf16[1,128,512]{2,1,0:T(8,128)(2,1)S(1)}, bf16[1,128,512]{2,1,0:T(8,128)(2,1)S(1)}, u32[]{:S(2)}, u32[]{:S(2)}) %collective-permute-start.20) | collective-permute-done | bytes 131104 | tf_op jit(solution)/shard_map/ppermute | solution.py:18
  33.4 1.9 %collective-permute-done.25.refs_4_ = bf16[1,128,512]{2,1,0:T(8,128)(2,1)S(1)} collective-permute-done((bf16[1,128,512]{2,1,0:T(8,128)(2,1)S(1)}, bf16[1,128,512]{2,1,0:T(8,128)(2,1)S(1)}, u32[]{:S(2)}, u32[]{:S(2)}) %collective-permute-start.25) | collective-permute-done | bytes 131104 | tf_op jit(solution)/shard_map/ppermute | solution.py:18
  35.5 1.4 %collective-permute-start.26 = (bf16[1,128,512]{2,1,0:T(8,128)(2,1)S(1)}, bf16[1,128,512]{2,1,0:T(8,128)(2,1)S(1)}, u32[]{:S(2)}, u32[]{:S(2)}) collective-permute-start(bf16[1,128,512]{2,1,0:T(8,128)(2,1)S(1)} %get-tuple-element.31.refs_0_), channel_id=1, source_target_pairs={{0,8},{1,9},{2,10},{3,11},{4,12},{5,13},{6,14},{7,15},{8,0},{9,1},... | collective-permute-start | bytes 393224 | tf_op jit(solution)/shard_map/ppermute | solution.py:18
  37.0 1.7 %collective-permute-start.4 = (bf16[1,128,512]{2,1,0:T(8,128)(2,1)S(1)}, bf16[1,128,512]{2,1,0:T(8,128)(2,1)S(1)}, u32[]{:S(2)}, u32[]{:S(2)}) collective-permute-start(bf16[1,128,512]{2,1,0:T(8,128)(2,1)S(1)} %shard_map.132), channel_id=1, source_target_pairs={{0,8},{1,9},{2,10},{3,11},{4,12},{5,13},{6,14},{7,15},{8,0},{9,1},... | collective-permute-start | bytes 393224 | tf_op jit(solution)/shard_map/ppermute | solution.py:18
  38.9 6.4 %collective-permute-done.26.refs_1_.refs_2_ = bf16[1,128,512]{2,1,0:T(8,128)(2,1)S(1)} collective-permute-done((bf16[1,128,512]{2,1,0:T(8,128)(2,1)S(1)}, bf16[1,128,512]{2,1,0:T(8,128)(2,1)S(1)}, u32[]{:S(2)}, u32[]{:S(2)}) %collective-permute-start.26) | collective-permute-done | bytes 131104 | tf_op jit(solution)/shard_map/ppermute | solution.py:18
  45.3 1.4 %collective-permute-done.4.refs_4_ = bf16[1,128,512]{2,1,0:T(8,128)(2,1)S(1)} collective-permute-done((bf16[1,128,512]{2,1,0:T(8,128)(2,1)S(1)}, bf16[1,128,512]{2,1,0:T(8,128)(2,1)S(1)}, u32[]{:S(2)}, u32[]{:S(2)}) %collective-permute-start.4) | collective-permute-done | bytes 131104 | tf_op jit(solution)/shard_map/ppermute | solution.py:18
  46.9 1.6 %collective-permute-start.10 = (bf16[1,128,512]{2,1,0:T(8,128)(2,1)S(1)}, bf16[1,128,512]{2,1,0:T(8,128)(2,1)S(1)}, u32[]{:S(2)}, u32[]{:S(2)}) collective-permute-start(bf16[1,128,512]{2,1,0:T(8,128)(2,1)S(1)} %get-tuple-element.26.refs_0_), channel_id=1, source_target_pairs={{0,2},{1,3},{2,0},{3,1},{4,6},{5,7},{6,4},{7,5},{8,10},{9,11},{10,... | collective-permute-start | bytes 393224 | tf_op jit(solution)/shard_map/ppermute | solution.py:18
  48.5 0.9 %collective-permute-start.32 = (bf16[2,128,512]{2,1,0:T(8,128)(2,1)S(1)}, bf16[2,128,512]{2,1,0:T(8,128)(2,1)S(1)}, u32[]{:S(2)}, u32[]{:S(2)}) collective-permute-start(bf16[2,128,512]{2,1,0:T(8,128)(2,1)S(1)} %shard_map.150), channel_id=1, source_target_pairs={{0,2},{1,3},{2,0},{3,1},{4,6},{5,7},{6,4},{7,5},{8,10},{9,11},{10,... | collective-permute-start | bytes 786440 | tf_op jit(solution)/shard_map/ppermute | solution.py:18
  49.4 1.6 %collective-permute-start.5 = (bf16[1,128,512]{2,1,0:T(8,128)(2,1)S(1)}, bf16[1,128,512]{2,1,0:T(8,128)(2,1)S(1)}, u32[]{:S(2)}, u32[]{:S(2)}) collective-permute-start(bf16[1,128,512]{2,1,0:T(8,128)(2,1)S(1)} %get-tuple-element.26.refs_0_), channel_id=1, source_target_pairs={{0,8},{1,9},{2,10},{3,11},{4,12},{5,13},{6,14},{7,15},{8,0},{9,1},... | collective-permute-start | bytes 393224 | tf_op jit(solution)/shard_map/ppermute | solution.py:18
  51.0 1.4 %collective-permute-start.34 = (bf16[1,128,512]{2,1,0:T(8,128)(2,1)S(1)}, bf16[1,128,512]{2,1,0:T(8,128)(2,1)S(1)}, u32[]{:S(2)}, u32[]{:S(2)}) collective-permute-start(bf16[1,128,512]{2,1,0:T(8,128)(2,1)S(1)} %get-tuple-element.31.refs_0_), channel_id=1, source_target_pairs={{0,2},{1,3},{2,0},{3,1},{4,6},{5,7},{6,4},{7,5},{8,10},{9,11},{10,... | collective-permute-start | bytes 393224 | tf_op jit(solution)/shard_map/ppermute | solution.py:18
  52.5 0.9 %collective-permute-done.10.refs_0_.refs_2_ = bf16[1,128,512]{2,1,0:T(8,128)(2,1)S(1)} collective-permute-done((bf16[1,128,512]{2,1,0:T(8,128)(2,1)S(1)}, bf16[1,128,512]{2,1,0:T(8,128)(2,1)S(1)}, u32[]{:S(2)}, u32[]{:S(2)}) %collective-permute-start.10) | collective-permute-done | bytes 131104 | tf_op jit(solution)/shard_map/ppermute | solution.py:18
  53.4 3.3 %collective-permute-done.5.refs_1_.refs_2_ = bf16[1,128,512]{2,1,0:T(8,128)(2,1)S(1)} collective-permute-done((bf16[1,128,512]{2,1,0:T(8,128)(2,1)S(1)}, bf16[1,128,512]{2,1,0:T(8,128)(2,1)S(1)}, u32[]{:S(2)}, u32[]{:S(2)}) %collective-permute-start.5) | collective-permute-done | bytes 131104 | tf_op jit(solution)/shard_map/ppermute | solution.py:18
  56.7 1.2 %collective-permute-start.28 = (bf16[1,128,512]{2,1,0:T(8,128)(2,1)S(1)}, bf16[1,128,512]{2,1,0:T(8,128)(2,1)S(1)}, u32[]{:S(2)}, u32[]{:S(2)}) collective-permute-start(bf16[1,128,512]{2,1,0:T(8,128)(2,1)S(1)} %collective-permute-done.27.refs_0_), channel_id=1, source_target_pairs={{0,2},{1,3},{2,0},{3,1},{4,6},{5,7},{6,4},{7,5},{8,10},{9,11},{10,... | collective-permute-start | bytes 393224 | tf_op jit(solution)/shard_map/ppermute | solution.py:18
  57.9 2.5 %collective-permute-done.34.refs_0_ = bf16[1,128,512]{2,1,0:T(8,128)(2,1)S(1)} collective-permute-done((bf16[1,128,512]{2,1,0:T(8,128)(2,1)S(1)}, bf16[1,128,512]{2,1,0:T(8,128)(2,1)S(1)}, u32[]{:S(2)}, u32[]{:S(2)}) %collective-permute-start.34) | collective-permute-done | bytes 131104 | tf_op jit(solution)/shard_map/ppermute | solution.py:18
  60.6 0.5 collective-permute-start.30
  61.2 0.6 collective-permute-done.28.refs_0_
  62.3 1.6 %collective-permute-start.13 = (bf16[1,128,512]{2,1,0:T(8,128)(2,1)S(1)}, bf16[1,128,512]{2,1,0:T(8,128)(2,1)S(1)}, u32[]{:S(2)}, u32[]{:S(2)}) collective-permute-start(bf16[1,128,512]{2,1,0:T(8,128)(2,1)S(1)} %get-tuple-element.26.refs_0_), channel_id=1, source_target_pairs={{0,4},{1,5},{2,6},{3,7},{4,0},{5,1},{6,2},{7,3},{8,12},{9,13},{10,... | collective-permute-start | bytes 393224 | tf_op jit(solution)/shard_map/ppermute | solution.py:18
  64.0 1.5 %collective-permute-start.6 = (bf16[1,128,512]{2,1,0:T(8,128)(2,1)S(1)}, bf16[1,128,512]{2,1,0:T(8,128)(2,1)S(1)}, u32[]{:S(2)}, u32[]{:S(2)}) collective-permute-start(bf16[1,128,512]{2,1,0:T(8,128)(2,1)S(1)} %collective-permute-done.5.refs_1_.refs_2_), channel_id=1, source_target_pairs={{0,2},{1,3},{2,0},{3,1},{4,6},{5,7},{6,4},{7,5},{8,10},{9,11},{10,... | collective-permute-start | bytes 393224 | tf_op jit(solution)/shard_map/ppermute | solution.py:18
  65.5 2.4 %shard_map.127.tokens = bf16[1024,2048]{1,0:T(8,128)(2,1)S(1)} custom-call(bf16[1024,2048]{1,0:T(8,128)(2,1)} %tokens.1), custom_call_target="tpu_custom_call" | custom-call | flops 1000000 | bytes 1000000 | tf_op jit(solution)/shard_map/pallas_call | solution.py:30
  67.9 0.9 %shard_map.158 = (f32[128,512]{1,0:T(8,128)}, f32[128,512]{1,0:T(8,128)}) custom-call(f32[1,2]{1,0:T(1,128)S(1)} %bitcast.5, f32[128,512]{1,0:T(8,128)S(1)} %copy-done, f32[128,512]{1,0:T(8,128)S(1)} %copy-done.1, f32[128,512]{1,0:T(8,128)S(1)} %get-tuple-element.35.summed), custom_call_target="tpu_custom_call" | custom-call | flops 1000000 | bytes 1000000 | tf_op jit(solution)/shard_map/pallas_call | solution.py:30
  68.8 0.7 shard_map.151.refs_4_
  69.5 0.6 collective-permute-start.17
  70.1 0.7 shard_map.152.refs_2_
  70.8 0.9 %shard_map.157 = (f32[128,512]{1,0:T(8,128)}, f32[128,512]{1,0:T(8,128)}) custom-call(f32[1,2]{1,0:T(1,128)S(1)} %bitcast.6, f32[128,512]{1,0:T(8,128)S(1)} %copy-done.2, f32[128,512]{1,0:T(8,128)S(1)} %copy-done.3, f32[128,512]{1,0:T(8,128)S(1)} %get-tuple-element.32.summed), custom_call_target="tpu_custom_call" | custom-call | flops 1000000 | bytes 1000000 | tf_op jit(solution)/shard_map/pallas_call | solution.py:30
  71.7 0.5 collective-permute-start.14
  72.2 0.7 collective-permute-start.7
  73.0 0.7 shard_map.153.refs_2_
  73.7 0.4 shard_map.154.refs_1_
  74.6 1.4 %shard_map.156 = bf16[1024,512]{1,0:T(8,128)(2,1)} custom-call(bf16[1024,2048]{1,0:T(8,128)(2,1)S(1)} %shard_map.127.tokens, bf16[1,128,512]{2,1,0:T(8,128)(2,1)S(1)} %collective-permute-done.29.refs_0_, f32[1024,512]{1,0:T(8,128)S(1)} %shard_map.155.refs_1_), custom_call_target="tpu_custom_call" | custom-call | flops 134217728 | bytes 1000000 | tf_op jit(solution)/shard_map/pallas_call | solution.py:30
  76.0 0.7 shard_map.135.refs_4_
  76.7 1.0 %collective-permute-done.7.refs_0_ = bf16[1,128,512]{2,1,0:T(8,128)(2,1)S(1)} collective-permute-done((bf16[1,128,512]{2,1,0:T(8,128)(2,1)S(1)}, bf16[1,128,512]{2,1,0:T(8,128)(2,1)S(1)}, u32[]{:S(2)}, u32[]{:S(2)}) %collective-permute-start.7) | collective-permute-done | bytes 131104 | tf_op jit(solution)/shard_map/ppermute | solution.py:18
  77.7 0.7 shard_map.136.refs_2_
  78.5 0.7 shard_map.137.refs_2_
  80.1 1.4 %shard_map.140 = bf16[1024,512]{1,0:T(8,128)(2,1)} custom-call(bf16[1024,2048]{1,0:T(8,128)(2,1)S(1)} %shard_map.127.tokens, bf16[1,128,512]{2,1,0:T(8,128)(2,1)S(1)} %collective-permute-done.8.refs_0_, f32[1024,512]{1,0:T(8,128)S(1)} %shard_map.139.refs_1_), custom_call_target="tpu_custom_call" | custom-call | flops 134217728 | bytes 1000000 | tf_op jit(solution)/shard_map/pallas_call | solution.py:30
  (72 shorter events, 3.9 us)
Async XLA Ops:
  2.0 5.4 %collective-permute-start.1 = (bf16[4,128,512]{2,1,0:T(8,128)(2,1)S(1)}, bf16[4,128,512]{2,1,0:T(8,128)(2,1)S(1)}, u32[]{:S(2)}, u32[]{:S(2)}) collective-permute-start(bf16[4,128,512]{2,1,0:T(8,128)(2,1)S(1)} %get-tuple-element.25), channel_id=1, source_target_pairs={{0,1},{1,0},{2,3},{3,2},{4,5},{5,4},{6,7},{7,6},{8,9},{9,8},{10,11... | collective-permute-start | bytes 1572872 | tf_op jit(solution)/shard_map/ppermute | solution.py:18
  3.9 6.7 %collective-permute-start.19 = (bf16[4,128,512]{2,1,0:T(8,128)(2,1)S(1)}, bf16[4,128,512]{2,1,0:T(8,128)(2,1)S(1)}, u32[]{:S(2)}, u32[]{:S(2)}) collective-permute-start(bf16[4,128,512]{2,1,0:T(8,128)(2,1)S(1)} %get-tuple-element.30), channel_id=1, source_target_pairs={{0,1},{1,0},{2,3},{3,2},{4,5},{5,4},{6,7},{7,6},{8,9},{9,8},{10,11... | collective-permute-start | bytes 1572872 | tf_op jit(solution)/shard_map/ppermute | solution.py:18
  5.4 7.5 %collective-permute-start.18 = (bf16[4,128,512]{2,1,0:T(8,128)(2,1)S(1)}, bf16[4,128,512]{2,1,0:T(8,128)(2,1)S(1)}, u32[]{:S(2)}, u32[]{:S(2)}) collective-permute-start(bf16[4,128,512]{2,1,0:T(8,128)(2,1)S(1)} %get-tuple-element.28), channel_id=1, source_target_pairs={{0,1},{1,0},{2,3},{3,2},{4,5},{5,4},{6,7},{7,6},{8,9},{9,8},{10,11... | collective-permute-start | bytes 1572872 | tf_op jit(solution)/shard_map/ppermute | solution.py:18
  7.3 12.8 %collective-permute-start = (bf16[4,128,512]{2,1,0:T(8,128)(2,1)S(1)}, bf16[4,128,512]{2,1,0:T(8,128)(2,1)S(1)}, u32[]{:S(2)}, u32[]{:S(2)}) collective-permute-start(bf16[4,128,512]{2,1,0:T(8,128)(2,1)S(1)} %get-tuple-element.23), channel_id=1, source_target_pairs={{0,1},{1,0},{2,3},{3,2},{4,5},{5,4},{6,7},{7,6},{8,9},{9,8},{10,11... | collective-permute-start | bytes 1572872 | tf_op jit(solution)/shard_map/ppermute | solution.py:18
  7.5 15.9 %collective-permute-start.2 = (bf16[4,128,512]{2,1,0:T(8,128)(2,1)S(1)}, bf16[4,128,512]{2,1,0:T(8,128)(2,1)S(1)}, u32[]{:S(2)}, u32[]{:S(2)}) collective-permute-start(bf16[4,128,512]{2,1,0:T(8,128)(2,1)S(1)} %shard_map.130), channel_id=1, source_target_pairs={{0,4},{1,5},{2,6},{3,7},{4,0},{5,1},{6,2},{7,3},{8,12},{9,13},{10,... | collective-permute-start | bytes 1572872 | tf_op jit(solution)/shard_map/ppermute | solution.py:18
  10.7 9.2 %collective-permute-start.23 = (bf16[2,128,512]{2,1,0:T(8,128)(2,1)S(1)}, bf16[2,128,512]{2,1,0:T(8,128)(2,1)S(1)}, u32[]{:S(2)}, u32[]{:S(2)}) collective-permute-start(bf16[2,128,512]{2,1,0:T(8,128)(2,1)S(1)} %shard_map.146), channel_id=1, source_target_pairs={{0,2},{1,3},{2,0},{3,1},{4,6},{5,7},{6,4},{7,5},{8,10},{9,11},{10,... | collective-permute-start | bytes 786440 | tf_op jit(solution)/shard_map/ppermute | solution.py:18
  12.3 13.4 %collective-permute-start.21 = (bf16[1,128,512]{2,1,0:T(8,128)(2,1)S(1)}, bf16[1,128,512]{2,1,0:T(8,128)(2,1)S(1)}, u32[]{:S(2)}, u32[]{:S(2)}) collective-permute-start(bf16[1,128,512]{2,1,0:T(8,128)(2,1)S(1)} %shard_map.144), channel_id=1, source_target_pairs={{0,2},{1,3},{2,0},{3,1},{4,6},{5,7},{6,4},{7,5},{8,10},{9,11},{10,... | collective-permute-start | bytes 393224 | tf_op jit(solution)/shard_map/ppermute | solution.py:18
  20.0 7.9 %collective-permute-start.24 = (bf16[1,128,512]{2,1,0:T(8,128)(2,1)S(1)}, bf16[1,128,512]{2,1,0:T(8,128)(2,1)S(1)}, u32[]{:S(2)}, u32[]{:S(2)}) collective-permute-start(bf16[1,128,512]{2,1,0:T(8,128)(2,1)S(1)} %shard_map.147), channel_id=1, source_target_pairs={{0,4},{1,5},{2,6},{3,7},{4,0},{5,1},{6,2},{7,3},{8,12},{9,13},{10,... | collective-permute-start | bytes 393224 | tf_op jit(solution)/shard_map/ppermute | solution.py:18
  23.5 11.8 %copy-start = (f32[128,512]{1,0:T(8,128)S(1)}, f32[128,512]{1,0:T(8,128)}, u32[]{:S(2)}) copy-start(f32[128,512]{1,0:T(8,128)} %master.7) | copy-start | bytes 786436
  23.5 11.8 %copy-start.1 = (f32[128,512]{1,0:T(8,128)S(1)}, f32[128,512]{1,0:T(8,128)}, u32[]{:S(2)}) copy-start(f32[128,512]{1,0:T(8,128)} %moment.7) | copy-start | bytes 786436
  23.5 11.8 %copy-start.4 = (f32[2]{0:T(128)S(1)}, f32[2]{0:T(128)}, u32[]{:S(2)}) copy-start(f32[2]{0:T(128)} %param.15) | copy-start | bytes 28
  23.5 13.4 %collective-permute-start.3 = (bf16[2,128,512]{2,1,0:T(8,128)(2,1)S(1)}, bf16[2,128,512]{2,1,0:T(8,128)(2,1)S(1)}, u32[]{:S(2)}, u32[]{:S(2)}) collective-permute-start(bf16[2,128,512]{2,1,0:T(8,128)(2,1)S(1)} %shard_map.131), channel_id=1, source_target_pairs={{0,2},{1,3},{2,0},{3,1},{4,6},{5,7},{6,4},{7,5},{8,10},{9,11},{10,... | collective-permute-start | bytes 786440 | tf_op jit(solution)/shard_map/ppermute | solution.py:18
  25.6 7.8 %collective-permute-start.20 = (bf16[1,128,512]{2,1,0:T(8,128)(2,1)S(1)}, bf16[1,128,512]{2,1,0:T(8,128)(2,1)S(1)}, u32[]{:S(2)}, u32[]{:S(2)}) collective-permute-start(bf16[1,128,512]{2,1,0:T(8,128)(2,1)S(1)} %shard_map.143), channel_id=1, source_target_pairs={{0,2},{1,3},{2,0},{3,1},{4,6},{5,7},{6,4},{7,5},{8,10},{9,11},{10,... | collective-permute-start | bytes 393224 | tf_op jit(solution)/shard_map/ppermute | solution.py:18
  25.8 7.6 %collective-permute-start.22 = (bf16[1,128,512]{2,1,0:T(8,128)(2,1)S(1)}, bf16[1,128,512]{2,1,0:T(8,128)(2,1)S(1)}, u32[]{:S(2)}, u32[]{:S(2)}) collective-permute-start(bf16[1,128,512]{2,1,0:T(8,128)(2,1)S(1)} %shard_map.145), channel_id=1, source_target_pairs={{0,4},{1,5},{2,6},{3,7},{4,0},{5,1},{6,2},{7,3},{8,12},{9,13},{10,... | collective-permute-start | bytes 393224 | tf_op jit(solution)/shard_map/ppermute | solution.py:18
  27.9 18.8 %copy-start.2 = (f32[128,512]{1,0:T(8,128)S(1)}, f32[128,512]{1,0:T(8,128)}, u32[]{:S(2)}) copy-start(f32[128,512]{1,0:T(8,128)} %master.6) | copy-start | bytes 786436
  28.0 18.7 %copy-start.3 = (f32[128,512]{1,0:T(8,128)S(1)}, f32[128,512]{1,0:T(8,128)}, u32[]{:S(2)}) copy-start(f32[128,512]{1,0:T(8,128)} %moment.6) | copy-start | bytes 786436
  28.0 7.3 %collective-permute-start.25 = (bf16[1,128,512]{2,1,0:T(8,128)(2,1)S(1)}, bf16[1,128,512]{2,1,0:T(8,128)(2,1)S(1)}, u32[]{:S(2)}, u32[]{:S(2)}) collective-permute-start(bf16[1,128,512]{2,1,0:T(8,128)(2,1)S(1)} %shard_map.148), channel_id=1, source_target_pairs={{0,8},{1,9},{2,10},{3,11},{4,12},{5,13},{6,14},{7,15},{8,0},{9,1},... | collective-permute-start | bytes 393224 | tf_op jit(solution)/shard_map/ppermute | solution.py:18
  35.5 9.7 %collective-permute-start.26 = (bf16[1,128,512]{2,1,0:T(8,128)(2,1)S(1)}, bf16[1,128,512]{2,1,0:T(8,128)(2,1)S(1)}, u32[]{:S(2)}, u32[]{:S(2)}) collective-permute-start(bf16[1,128,512]{2,1,0:T(8,128)(2,1)S(1)} %get-tuple-element.31.refs_0_), channel_id=1, source_target_pairs={{0,8},{1,9},{2,10},{3,11},{4,12},{5,13},{6,14},{7,15},{8,0},{9,1},... | collective-permute-start | bytes 393224 | tf_op jit(solution)/shard_map/ppermute | solution.py:18
  37.0 9.7 %collective-permute-start.4 = (bf16[1,128,512]{2,1,0:T(8,128)(2,1)S(1)}, bf16[1,128,512]{2,1,0:T(8,128)(2,1)S(1)}, u32[]{:S(2)}, u32[]{:S(2)}) collective-permute-start(bf16[1,128,512]{2,1,0:T(8,128)(2,1)S(1)} %shard_map.132), channel_id=1, source_target_pairs={{0,8},{1,9},{2,10},{3,11},{4,12},{5,13},{6,14},{7,15},{8,0},{9,1},... | collective-permute-start | bytes 393224 | tf_op jit(solution)/shard_map/ppermute | solution.py:18
  38.7 9.8 %collective-permute-start.31 = (bf16[1,128,512]{2,1,0:T(8,128)(2,1)S(1)}, bf16[1,128,512]{2,1,0:T(8,128)(2,1)S(1)}, u32[]{:S(2)}, u32[]{:S(2)}) collective-permute-start(bf16[1,128,512]{2,1,0:T(8,128)(2,1)S(1)} %get-tuple-element.31.refs_0_), channel_id=1, source_target_pairs={{0,4},{1,5},{2,6},{3,7},{4,0},{5,1},{6,2},{7,3},{8,12},{9,13},{10,... | collective-permute-start | bytes 393224 | tf_op jit(solution)/shard_map/ppermute | solution.py:18
  38.9 12.2 %collective-permute-start.37 = (bf16[1,128,512]{2,1,0:T(8,128)(2,1)S(1)}, bf16[1,128,512]{2,1,0:T(8,128)(2,1)S(1)}, u32[]{:S(2)}, u32[]{:S(2)}) collective-permute-start(bf16[1,128,512]{2,1,0:T(8,128)(2,1)S(1)} %get-tuple-element.31.refs_0_), channel_id=1, source_target_pairs={{0,1},{1,0},{2,3},{3,2},{4,5},{5,4},{6,7},{7,6},{8,9},{9,8},{10,11... | collective-permute-start | bytes 393224 | tf_op jit(solution)/shard_map/ppermute | solution.py:18
  45.3 7.2 %collective-permute-start.27 = (bf16[1,128,512]{2,1,0:T(8,128)(2,1)S(1)}, bf16[1,128,512]{2,1,0:T(8,128)(2,1)S(1)}, u32[]{:S(2)}, u32[]{:S(2)}) collective-permute-start(bf16[1,128,512]{2,1,0:T(8,128)(2,1)S(1)} %collective-permute-done.26.refs_1_.refs_2_), channel_id=1, source_target_pairs={{0,4},{1,5},{2,6},{3,7},{4,0},{5,1},{6,2},{7,3},{8,12},{9,13},{10,... | collective-permute-start | bytes 393224 | tf_op jit(solution)/shard_map/ppermute | solution.py:18
  46.9 6.4 %collective-permute-start.10 = (bf16[1,128,512]{2,1,0:T(8,128)(2,1)S(1)}, bf16[1,128,512]{2,1,0:T(8,128)(2,1)S(1)}, u32[]{:S(2)}, u32[]{:S(2)}) collective-permute-start(bf16[1,128,512]{2,1,0:T(8,128)(2,1)S(1)} %get-tuple-element.26.refs_0_), channel_id=1, source_target_pairs={{0,2},{1,3},{2,0},{3,1},{4,6},{5,7},{6,4},{7,5},{8,10},{9,11},{10,... | collective-permute-start | bytes 393224 | tf_op jit(solution)/shard_map/ppermute | solution.py:18
  48.5 12.6 %collective-permute-start.32 = (bf16[2,128,512]{2,1,0:T(8,128)(2,1)S(1)}, bf16[2,128,512]{2,1,0:T(8,128)(2,1)S(1)}, u32[]{:S(2)}, u32[]{:S(2)}) collective-permute-start(bf16[2,128,512]{2,1,0:T(8,128)(2,1)S(1)} %shard_map.150), channel_id=1, source_target_pairs={{0,2},{1,3},{2,0},{3,1},{4,6},{5,7},{6,4},{7,5},{8,10},{9,11},{10,... | collective-permute-start | bytes 786440 | tf_op jit(solution)/shard_map/ppermute | solution.py:18
  49.4 7.3 %collective-permute-start.5 = (bf16[1,128,512]{2,1,0:T(8,128)(2,1)S(1)}, bf16[1,128,512]{2,1,0:T(8,128)(2,1)S(1)}, u32[]{:S(2)}, u32[]{:S(2)}) collective-permute-start(bf16[1,128,512]{2,1,0:T(8,128)(2,1)S(1)} %get-tuple-element.26.refs_0_), channel_id=1, source_target_pairs={{0,8},{1,9},{2,10},{3,11},{4,12},{5,13},{6,14},{7,15},{8,0},{9,1},... | collective-permute-start | bytes 393224 | tf_op jit(solution)/shard_map/ppermute | solution.py:18
  51.0 9.4 %collective-permute-start.34 = (bf16[1,128,512]{2,1,0:T(8,128)(2,1)S(1)}, bf16[1,128,512]{2,1,0:T(8,128)(2,1)S(1)}, u32[]{:S(2)}, u32[]{:S(2)}) collective-permute-start(bf16[1,128,512]{2,1,0:T(8,128)(2,1)S(1)} %get-tuple-element.31.refs_0_), channel_id=1, source_target_pairs={{0,2},{1,3},{2,0},{3,1},{4,6},{5,7},{6,4},{7,5},{8,10},{9,11},{10,... | collective-permute-start | bytes 393224 | tf_op jit(solution)/shard_map/ppermute | solution.py:18
  52.5 8.2 %collective-permute-start.38 = (bf16[1,128,512]{2,1,0:T(8,128)(2,1)S(1)}, bf16[1,128,512]{2,1,0:T(8,128)(2,1)S(1)}, u32[]{:S(2)}, u32[]{:S(2)}) collective-permute-start(bf16[1,128,512]{2,1,0:T(8,128)(2,1)S(1)} %collective-permute-done.31.refs_0_.refs_2_), channel_id=1, source_target_pairs={{0,1},{1,0},{2,3},{3,2},{4,5},{5,4},{6,7},{7,6},{8,9},{9,8},{10,11... | collective-permute-start | bytes 393224 | tf_op jit(solution)/shard_map/ppermute | solution.py:18
  53.4 7.3 %collective-permute-start.36 = (bf16[1,128,512]{2,1,0:T(8,128)(2,1)S(1)}, bf16[1,128,512]{2,1,0:T(8,128)(2,1)S(1)}, u32[]{:S(2)}, u32[]{:S(2)}) collective-permute-start(bf16[1,128,512]{2,1,0:T(8,128)(2,1)S(1)} %collective-permute-done.26.refs_1_.refs_2_), channel_id=1, source_target_pairs={{0,1},{1,0},{2,3},{3,2},{4,5},{5,4},{6,7},{7,6},{8,9},{9,8},{10,11... | collective-permute-start | bytes 393224 | tf_op jit(solution)/shard_map/ppermute | solution.py:18
  56.7 5.1 %collective-permute-start.28 = (bf16[1,128,512]{2,1,0:T(8,128)(2,1)S(1)}, bf16[1,128,512]{2,1,0:T(8,128)(2,1)S(1)}, u32[]{:S(2)}, u32[]{:S(2)}) collective-permute-start(bf16[1,128,512]{2,1,0:T(8,128)(2,1)S(1)} %collective-permute-done.27.refs_0_), channel_id=1, source_target_pairs={{0,2},{1,3},{2,0},{3,1},{4,6},{5,7},{6,4},{7,5},{8,10},{9,11},{10,... | collective-permute-start | bytes 393224 | tf_op jit(solution)/shard_map/ppermute | solution.py:18
  60.4 8.4 %collective-permute-start.11 = (bf16[2,128,512]{2,1,0:T(8,128)(2,1)S(1)}, bf16[2,128,512]{2,1,0:T(8,128)(2,1)S(1)}, u32[]{:S(2)}, u32[]{:S(2)}) collective-permute-start(bf16[2,128,512]{2,1,0:T(8,128)(2,1)S(1)} %shard_map.134), channel_id=1, source_target_pairs={{0,4},{1,5},{2,6},{3,7},{4,0},{5,1},{6,2},{7,3},{8,12},{9,13},{10,... | collective-permute-start | bytes 786440 | tf_op jit(solution)/shard_map/ppermute | solution.py:18
  60.6 1.3 %collective-permute-start.35 = (bf16[1,128,512]{2,1,0:T(8,128)(2,1)S(1)}, bf16[1,128,512]{2,1,0:T(8,128)(2,1)S(1)}, u32[]{:S(2)}, u32[]{:S(2)}) collective-permute-start(bf16[1,128,512]{2,1,0:T(8,128)(2,1)S(1)} %collective-permute-done.34.refs_0_), channel_id=1, source_target_pairs={{0,1},{1,0},{2,3},{3,2},{4,5},{5,4},{6,7},{7,6},{8,9},{9,8},{10,11... | collective-permute-start | bytes 393224 | tf_op jit(solution)/shard_map/ppermute | solution.py:18
  60.6 1.7 %collective-permute-start.30 = (bf16[1,128,512]{2,1,0:T(8,128)(2,1)S(1)}, bf16[1,128,512]{2,1,0:T(8,128)(2,1)S(1)}, u32[]{:S(2)}, u32[]{:S(2)}) collective-permute-start(bf16[1,128,512]{2,1,0:T(8,128)(2,1)S(1)} %collective-permute-done.27.refs_0_), channel_id=1, source_target_pairs={{0,1},{1,0},{2,3},{3,2},{4,5},{5,4},{6,7},{7,6},{8,9},{9,8},{10,11... | collective-permute-start | bytes 393224 | tf_op jit(solution)/shard_map/ppermute | solution.py:18
  61.2 10.6 %collective-permute-start.33 = (bf16[2,128,512]{2,1,0:T(8,128)(2,1)S(1)}, bf16[2,128,512]{2,1,0:T(8,128)(2,1)S(1)}, u32[]{:S(2)}, u32[]{:S(2)}) collective-permute-start(bf16[2,128,512]{2,1,0:T(8,128)(2,1)S(1)} %collective-permute-done.32.refs_0_), channel_id=1, source_target_pairs={{0,1},{1,0},{2,3},{3,2},{4,5},{5,4},{6,7},{7,6},{8,9},{9,8},{10,11... | collective-permute-start | bytes 786440 | tf_op jit(solution)/shard_map/ppermute | solution.py:18
  61.8 2.2 %collective-permute-start.29 = (bf16[1,128,512]{2,1,0:T(8,128)(2,1)S(1)}, bf16[1,128,512]{2,1,0:T(8,128)(2,1)S(1)}, u32[]{:S(2)}, u32[]{:S(2)}) collective-permute-start(bf16[1,128,512]{2,1,0:T(8,128)(2,1)S(1)} %collective-permute-done.28.refs_0_), channel_id=1, source_target_pairs={{0,1},{1,0},{2,3},{3,2},{4,5},{5,4},{6,7},{7,6},{8,9},{9,8},{10,11... | collective-permute-start | bytes 393224 | tf_op jit(solution)/shard_map/ppermute | solution.py:18
  62.0 7.5 %collective-permute-start.16 = (bf16[1,128,512]{2,1,0:T(8,128)(2,1)S(1)}, bf16[1,128,512]{2,1,0:T(8,128)(2,1)S(1)}, u32[]{:S(2)}, u32[]{:S(2)}) collective-permute-start(bf16[1,128,512]{2,1,0:T(8,128)(2,1)S(1)} %get-tuple-element.26.refs_0_), channel_id=1, source_target_pairs={{0,1},{1,0},{2,3},{3,2},{4,5},{5,4},{6,7},{7,6},{8,9},{9,8},{10,11... | collective-permute-start | bytes 393224 | tf_op jit(solution)/shard_map/ppermute | solution.py:18
  62.3 9.4 %collective-permute-start.13 = (bf16[1,128,512]{2,1,0:T(8,128)(2,1)S(1)}, bf16[1,128,512]{2,1,0:T(8,128)(2,1)S(1)}, u32[]{:S(2)}, u32[]{:S(2)}) collective-permute-start(bf16[1,128,512]{2,1,0:T(8,128)(2,1)S(1)} %get-tuple-element.26.refs_0_), channel_id=1, source_target_pairs={{0,4},{1,5},{2,6},{3,7},{4,0},{5,1},{6,2},{7,3},{8,12},{9,13},{10,... | collective-permute-start | bytes 393224 | tf_op jit(solution)/shard_map/ppermute | solution.py:18
  64.0 8.3 %collective-permute-start.6 = (bf16[1,128,512]{2,1,0:T(8,128)(2,1)S(1)}, bf16[1,128,512]{2,1,0:T(8,128)(2,1)S(1)}, u32[]{:S(2)}, u32[]{:S(2)}) collective-permute-start(bf16[1,128,512]{2,1,0:T(8,128)(2,1)S(1)} %collective-permute-done.5.refs_1_.refs_2_), channel_id=1, source_target_pairs={{0,2},{1,3},{2,0},{3,1},{4,6},{5,7},{6,4},{7,5},{8,10},{9,11},{10,... | collective-permute-start | bytes 393224 | tf_op jit(solution)/shard_map/ppermute | solution.py:18
  68.8 9.7 %collective-permute-start.12 = (bf16[2,128,512]{2,1,0:T(8,128)(2,1)S(1)}, bf16[2,128,512]{2,1,0:T(8,128)(2,1)S(1)}, u32[]{:S(2)}, u32[]{:S(2)}) collective-permute-start(bf16[2,128,512]{2,1,0:T(8,128)(2,1)S(1)} %collective-permute-done.11.refs_0_), channel_id=1, source_target_pairs={{0,1},{1,0},{2,3},{3,2},{4,5},{5,4},{6,7},{7,6},{8,9},{9,8},{10,11... | collective-permute-start | bytes 786440 | tf_op jit(solution)/shard_map/ppermute | solution.py:18
  69.5 6.4 %collective-permute-start.17 = (bf16[1,128,512]{2,1,0:T(8,128)(2,1)S(1)}, bf16[1,128,512]{2,1,0:T(8,128)(2,1)S(1)}, u32[]{:S(2)}, u32[]{:S(2)}) collective-permute-start(bf16[1,128,512]{2,1,0:T(8,128)(2,1)S(1)} %collective-permute-done.10.refs_0_.refs_2_), channel_id=1, source_target_pairs={{0,1},{1,0},{2,3},{3,2},{4,5},{5,4},{6,7},{7,6},{8,9},{9,8},{10,11... | collective-permute-start | bytes 393224 | tf_op jit(solution)/shard_map/ppermute | solution.py:18
  71.7 6.0 %collective-permute-start.15 = (bf16[1,128,512]{2,1,0:T(8,128)(2,1)S(1)}, bf16[1,128,512]{2,1,0:T(8,128)(2,1)S(1)}, u32[]{:S(2)}, u32[]{:S(2)}) collective-permute-start(bf16[1,128,512]{2,1,0:T(8,128)(2,1)S(1)} %collective-permute-done.5.refs_1_.refs_2_), channel_id=1, source_target_pairs={{0,1},{1,0},{2,3},{3,2},{4,5},{5,4},{6,7},{7,6},{8,9},{9,8},{10,11... | collective-permute-start | bytes 393224 | tf_op jit(solution)/shard_map/ppermute | solution.py:18
  71.7 6.0 %collective-permute-start.14 = (bf16[1,128,512]{2,1,0:T(8,128)(2,1)S(1)}, bf16[1,128,512]{2,1,0:T(8,128)(2,1)S(1)}, u32[]{:S(2)}, u32[]{:S(2)}) collective-permute-start(bf16[1,128,512]{2,1,0:T(8,128)(2,1)S(1)} %collective-permute-done.13.refs_0_), channel_id=1, source_target_pairs={{0,1},{1,0},{2,3},{3,2},{4,5},{5,4},{6,7},{7,6},{8,9},{9,8},{10,11... | collective-permute-start | bytes 393224 | tf_op jit(solution)/shard_map/ppermute | solution.py:18
  72.2 5.5 %collective-permute-start.7 = (bf16[1,128,512]{2,1,0:T(8,128)(2,1)S(1)}, bf16[1,128,512]{2,1,0:T(8,128)(2,1)S(1)}, u32[]{:S(2)}, u32[]{:S(2)}) collective-permute-start(bf16[1,128,512]{2,1,0:T(8,128)(2,1)S(1)} %collective-permute-done.6.refs_0_), channel_id=1, source_target_pairs={{0,4},{1,5},{2,6},{3,7},{4,0},{5,1},{6,2},{7,3},{8,12},{9,13},{10,... | collective-permute-start | bytes 393224 | tf_op jit(solution)/shard_map/ppermute | solution.py:18
  76.0 3.2 %collective-permute-start.9 = (bf16[1,128,512]{2,1,0:T(8,128)(2,1)S(1)}, bf16[1,128,512]{2,1,0:T(8,128)(2,1)S(1)}, u32[]{:S(2)}, u32[]{:S(2)}) collective-permute-start(bf16[1,128,512]{2,1,0:T(8,128)(2,1)S(1)} %collective-permute-done.6.refs_0_), channel_id=1, source_target_pairs={{0,1},{1,0},{2,3},{3,2},{4,5},{5,4},{6,7},{7,6},{8,9},{9,8},{10,11... | collective-permute-start | bytes 393224 | tf_op jit(solution)/shard_map/ppermute | solution.py:18
  77.7 2.3 %collective-permute-start.8 = (bf16[1,128,512]{2,1,0:T(8,128)(2,1)S(1)}, bf16[1,128,512]{2,1,0:T(8,128)(2,1)S(1)}, u32[]{:S(2)}, u32[]{:S(2)}) collective-permute-start(bf16[1,128,512]{2,1,0:T(8,128)(2,1)S(1)} %collective-permute-done.7.refs_0_), channel_id=1, source_target_pairs={{0,1},{1,0},{2,3},{3,2},{4,5},{5,4},{6,7},{7,6},{8,9},{9,8},{10,11... | collective-permute-start | bytes 393224 | tf_op jit(solution)/shard_map/ppermute | solution.py:18
where the time goes:
time: 81.7 us; the launch traced here: 81.5 us
  waiting for transfers between devices  31.4 us (38%)
  starting transfers between devices  29.6 us (36%)
  Pallas kernels  19.5 us (24%)
  between operations  0.89 us (1%)
    ppermute x39, waiting for transfers between devices, swap(): lax.ppermute(array, 'replica', [(r, r ^ stride) for r in range(replicas)])  31.4 us
    ppermute x39, starting transfers between devices, swap(): lax.ppermute(array, 'replica', [(r, r ^ stride) for r in range(replicas)])  29.6 us
    pallas_call x32, Pallas kernels, call(): pl.pallas_call(kernel, out_shape=[shape(*o) for o in out], in_specs=specs...  19.5 us
  transfers between devices with their start and end apart: 39, of which 12 were waited for; matrix products, arithmetic and copies ran while one was open for 0% of the time, Pallas kernels for 21%

commit v1 on v0

--- a/solution.py
+++ b/solution.py
@@ -34,7 +34,7 @@
         out_specs=[IN_VMEM] * len(out),
         scratch_shapes=scratch,
         cost_estimate=pl.CostEstimate(flops=flops, bytes_accessed=10**6, transcendentals=0),
-        compiler_params=pltpu.CompilerParams(vmem_limit_bytes=8 * 2**20),
+        compiler_params=pltpu.CompilerParams(vmem_limit_bytes=12 * 2**20),
         **options,
     )(*arrays)
 
@@ -89,14 +89,26 @@
     moment_out[...] = moment_new
 
 
+def product(height, blocks, tokens, slabs):
+    weights = jnp.concatenate([s[...].reshape(-1, s.shape[-1]) for s in slabs], axis=0)
+    rows = jnp.concatenate([tokens[:, k * height : (k + 1) * height] for k in blocks], axis=1)
+    return jnp.dot(rows, weights, preferred_element_type=F32)
+
+
 def product_kernel(height, blocks, groups, tokens, *refs):
     slabs, out = refs[:groups], refs[-1]
-    weights = jnp.concatenate([s[...].reshape(-1, s.shape[-1]) for s in slabs], axis=0)
-    rows = jnp.concatenate([tokens[:, k * height : (k + 1) * height] for k in blocks], axis=1)
-    total = jnp.dot(rows, weights, preferred_element_type=F32)
+    total = product(height, blocks, tokens, slabs)
     if len(refs) > groups + 1:
         total = total + refs[groups][...]
-    out[...] = total.astype(out.dtype)
+    out[...] = total
+
+
+def finish_kernel(height, plans, tokens, *refs):
+    refs, outs = refs[: -len(plans)], refs[-len(plans) :]
+    step = len(refs) // len(plans)
+    for n, (blocks, out) in enumerate(zip(plans, outs)):
+        total, *slabs = refs[n * step : (n + 1) * step]
+        out[...] = (total[...] + product(height, blocks, tokens, slabs)).astype(out.dtype)
 
 
 def columns_kernel(rows, tokens, out, sem):
@@ -116,12 +128,12 @@
 
 
 SUMS = {
-    "k": [(4, [4, 6, 12, 14]), (2, [2, 10]), (8, [8])],
-    "v": [(2, [2]), (2, [10, 14]), (2, [6]), (4, [4]), (4, [12]), (8, [8])],
+    "k": [(4, [12, 14]), (2, [2, 6]), (2, [10]), (4, [4]), (8, [8])],
+    "v": [(2, [2]), (2, [10]), (2, [6, 14]), (4, [4]), (4, [12]), (8, [8])],
 }
 GATHERS = {
-    "k": [(2, [2]), (4, [4]), (8, [8]), (4, [6, 12]), (2, [10]), (4, [14])],
-    "v": [(4, [4]), (2, [2]), (8, [8]), (2, [6, 10]), (4, [12]), (2, [14])],
+    "k": [(4, [4]), (8, [8]), (2, [2]), (4, [6, 12]), (2, [10]), (4, [14])],
+    "v": [(4, [4]), (2, [2]), (8, [8]), (4, [12]), (2, [6]), (2, [10]), (2, [14])],
 }
 
 
@@ -145,8 +157,7 @@
         if count >= 4:
             steps.append(step)
             step, count = [], 0
-    last = len(groups) - 1
-    return steps + ([step] if step else []) + [[(last, 0)], [(last, 1)]]
+    return steps + ([step] if step else [])
 
 
 def body(
@@ -255,20 +266,31 @@
                 whole = whole.at[me ^ jnp.array(blocks)].set(array)
             return jnp.dot(tokens, whole.reshape(-1, width), preferred_element_type=F32).astype(BF16)
         total = None
-        steps = steps_of(groups)
-        for i, step in enumerate(steps):
-            last = i == len(steps) - 1
+        for step in steps_of(groups):
             taken = [arrivals[n][side] for n, side in step]
             blocks = [b for part, _ in taken for b in part]
             arrays = [columns] + [array for _, array in taken] + ([] if total is None else [total])
             (total,) = call(
                 functools.partial(product_kernel, rows, blocks, len(step)),
                 arrays,
-                [((tokens.shape[0], width), BF16 if last else F32)],
+                [((tokens.shape[0], width), F32)],
                 flops=2 * tokens.shape[0] * len(blocks) * rows * width,
-                hold=not last,
             )
-        return total
+        return total, arrivals[-1]
+
+    def finish(parts):
+        if rows % 128:
+            return parts
+        plans = [[b for blocks, _ in taken for b in blocks] for _, taken in parts]
+        arrays = [columns]
+        for total, taken in parts:
+            arrays += [total] + [array for _, array in taken]
+        return call(
+            functools.partial(finish_kernel, rows, plans),
+            arrays,
+            [((tokens.shape[0], width), BF16)] * len(parts),
+            hold=False,
+        )
 
     def stream(pseudo, master, moment, s):
         sums = SUMS[s] if depth == 4 else plain_sums(depth)
@@ -276,9 +298,9 @@
         weights, state = weigh(reduce(pseudo, sums), master, moment)
         return project(*gather(weights, gathers)), state
 
-    projected_keys, state_k = stream(pseudo_keys, master_keys, moment_keys, "k")
-    projected_values, state_v = stream(pseudo_values, master_values, moment_values, "v")
-    return (projected_keys, projected_values, *state_k, *state_v)
+    product_k, state_k = stream(pseudo_keys, master_keys, moment_keys, "k")
+    product_v, state_v = stream(pseudo_values, master_values, moment_values, "v")
+    return (*finish([product_k, product_v]), *state_k, *state_v)
 
 
 def solution(mesh):

time: 81.7 us -> 82.2 us (level)
  starting transfers between devices: 29.6 us -> 33.8 us
  Pallas kernels: 19.5 us -> 17.6 us
  waiting for transfers between devices: 31.4 us -> 29.6 us
    ppermute x39 -> x43, starting transfers between devices: 29.6 us -> 33.8 us  [swap(): lax.ppermute(array, 'replica', [(r, r ^ stride) for r in range(replicas)])]
    pallas_call x32 -> x30, Pallas kernels: 19.5 us -> 17.6 us  [call(): pl.pallas_call(kernel, out_shape=[shape(*o) for o in out], in_specs=specs...]
    ppermute x39 -> x43, waiting for transfers between devices: 31.4 us -> 29.6 us  [swap(): lax.ppermute(array, 'replica', [(r, r ^ stride) for r in range(replicas)])]
  transfers between devices with their start and end apart: 39 -> 43, of which waited for: 12 -> 13; matrix products, arithmetic and copies ran while one was open for 0% -> 0% of each run, Pallas kernels for 21% -> 18%
where the time goes in v1:
time: 82.2 us; the launch traced here: 81.9 us
  starting transfers between devices  33.8 us (41%)
  waiting for transfers between devices  29.6 us (36%)
  Pallas kernels  17.6 us (21%)
  between operations  0.94 us (1%)
    ppermute x43, starting transfers between devices, swap(): lax.ppermute(array, 'replica', [(r, r ^ stride) for r in range(replicas)])  33.8 us
    ppermute x43, waiting for transfers between devices, swap(): lax.ppermute(array, 'replica', [(r, r ^ stride) for r in range(replicas)])  29.6 us
    pallas_call x30, Pallas kernels, call(): pl.pallas_call(kernel, out_shape=[shape(*o) for o in out], in_specs=specs...  17.6 us
  transfers between devices with their start and end apart: 43, of which 13 were waited for; matrix products, arithmetic and copies ran while one was open for 0% of the time, Pallas kernels for 18%

profile of v1, /device:TPU:0, one launch (start us, length us, event | category | flops | bytes accessed | tf_op | source)
XLA Modules:
  0.0 81.9 jit_solution(12582204352038011403)
XLA Ops:
  0.6 1.4 %shard_map.142 = (bf16[4,128,512]{2,1,0:T(8,128)(2,1)S(1)}, bf16[4,128,512]{2,1,0:T(8,128)(2,1)S(1)}) custom-call(bf16[16,128,512]{2,1,0:T(8,128)(2,1)} %bitcast.7), custom_call_target="tpu_custom_call" | custom-call | flops 1000000 | bytes 1000000 | tf_op jit(solution)/shard_map/pallas_call | solution.py:30
  2.0 0.6 collective-permute-start.21
  2.6 1.3 %shard_map.129 = (bf16[4,128,512]{2,1,0:T(8,128)(2,1)S(1)}, bf16[4,128,512]{2,1,0:T(8,128)(2,1)S(1)}) custom-call(bf16[16,128,512]{2,1,0:T(8,128)(2,1)} %bitcast.9), custom_call_target="tpu_custom_call" | custom-call | flops 1000000 | bytes 1000000 | tf_op jit(solution)/shard_map/pallas_call | solution.py:30
  4.0 1.3 %shard_map.141 = (bf16[4,128,512]{2,1,0:T(8,128)(2,1)S(1)}, bf16[4,128,512]{2,1,0:T(8,128)(2,1)S(1)}) custom-call(bf16[16,128,512]{2,1,0:T(8,128)(2,1)} %bitcast.8), custom_call_target="tpu_custom_call" | custom-call | flops 1000000 | bytes 1000000 | tf_op jit(solution)/shard_map/pallas_call | solution.py:30
  5.4 0.6 collective-permute-start.20
  5.9 1.3 %shard_map.128 = (bf16[4,128,512]{2,1,0:T(8,128)(2,1)S(1)}, bf16[4,128,512]{2,1,0:T(8,128)(2,1)S(1)}) custom-call(bf16[16,128,512]{2,1,0:T(8,128)(2,1)} %bitcast.10), custom_call_target="tpu_custom_call" | custom-call | flops 1000000 | bytes 1000000 | tf_op jit(solution)/shard_map/pallas_call | solution.py:30
  7.4 3.1 %collective-permute-start.23 = (bf16[2,128,512]{2,1,0:T(8,128)(2,1)S(1)}, bf16[2,128,512]{2,1,0:T(8,128)(2,1)S(1)}, u32[]{:S(2)}, u32[]{:S(2)}) collective-permute-start(bf16[2,128,512]{2,1,0:T(8,128)(2,1)S(1)} %shard_map.144), channel_id=1, source_target_pairs={{0,2},{1,3},{2,0},{3,1},{4,6},{5,7},{6,4},{7,5},{8,10},{9,11},{10,... | collective-permute-start | bytes 786440 | tf_op jit(solution)/shard_map/ppermute | solution.py:18
  10.5 1.6 %collective-permute-start.4 = (bf16[2,128,512]{2,1,0:T(8,128)(2,1)S(1)}, bf16[2,128,512]{2,1,0:T(8,128)(2,1)S(1)}, u32[]{:S(2)}, u32[]{:S(2)}) collective-permute-start(bf16[2,128,512]{2,1,0:T(8,128)(2,1)S(1)} %shard_map.132), channel_id=1, source_target_pairs={{0,4},{1,5},{2,6},{3,7},{4,0},{5,1},{6,2},{7,3},{8,12},{9,13},{10,... | collective-permute-start | bytes 786440 | tf_op jit(solution)/shard_map/ppermute | solution.py:18
  12.3 0.6 collective-permute-start.2
  12.9 1.6 %collective-permute-start.25 = (bf16[1,128,512]{2,1,0:T(8,128)(2,1)S(1)}, bf16[1,128,512]{2,1,0:T(8,128)(2,1)S(1)}, u32[]{:S(2)}, u32[]{:S(2)}) collective-permute-start(bf16[1,128,512]{2,1,0:T(8,128)(2,1)S(1)} %shard_map.146), channel_id=1, source_target_pairs={{0,2},{1,3},{2,0},{3,1},{4,6},{5,7},{6,4},{7,5},{8,10},{9,11},{10,... | collective-permute-start | bytes 393224 | tf_op jit(solution)/shard_map/ppermute | solution.py:18
  14.5 3.2 %collective-permute-done.23.refs_2_ = bf16[2,128,512]{2,1,0:T(8,128)(2,1)S(1)} collective-permute-done((bf16[2,128,512]{2,1,0:T(8,128)(2,1)S(1)}, bf16[2,128,512]{2,1,0:T(8,128)(2,1)S(1)}, u32[]{:S(2)}, u32[]{:S(2)}) %collective-permute-start.23) | collective-permute-done | bytes 262176 | tf_op jit(solution)/shard_map/ppermute | solution.py:18
  17.7 2.1 %collective-permute-start.26 = (bf16[1,128,512]{2,1,0:T(8,128)(2,1)S(1)}, bf16[1,128,512]{2,1,0:T(8,128)(2,1)S(1)}, u32[]{:S(2)}, u32[]{:S(2)}) collective-permute-start(bf16[1,128,512]{2,1,0:T(8,128)(2,1)S(1)} %shard_map.147), channel_id=1, source_target_pairs={{0,4},{1,5},{2,6},{3,7},{4,0},{5,1},{6,2},{7,3},{8,12},{9,13},{10,... | collective-permute-start | bytes 393224 | tf_op jit(solution)/shard_map/ppermute | solution.py:18
  19.9 1.6 %collective-permute-start.5 = (bf16[1,128,512]{2,1,0:T(8,128)(2,1)S(1)}, bf16[1,128,512]{2,1,0:T(8,128)(2,1)S(1)}, u32[]{:S(2)}, u32[]{:S(2)}) collective-permute-start(bf16[1,128,512]{2,1,0:T(8,128)(2,1)S(1)} %shard_map.133), channel_id=1, source_target_pairs={{0,2},{1,3},{2,0},{3,1},{4,6},{5,7},{6,4},{7,5},{8,10},{9,11},{10,... | collective-permute-start | bytes 393224 | tf_op jit(solution)/shard_map/ppermute | solution.py:18
  21.5 0.6 collective-permute-start.22
  22.2 3.9 %collective-permute-done.25.refs_2_ = bf16[1,128,512]{2,1,0:T(8,128)(2,1)S(1)} collective-permute-done((bf16[1,128,512]{2,1,0:T(8,128)(2,1)S(1)}, bf16[1,128,512]{2,1,0:T(8,128)(2,1)S(1)}, u32[]{:S(2)}, u32[]{:S(2)}) %collective-permute-start.25) | collective-permute-done | bytes 131104 | tf_op jit(solution)/shard_map/ppermute | solution.py:18
  26.1 2.1 %collective-permute-start.24 = (bf16[1,128,512]{2,1,0:T(8,128)(2,1)S(1)}, bf16[1,128,512]{2,1,0:T(8,128)(2,1)S(1)}, u32[]{:S(2)}, u32[]{:S(2)}) collective-permute-start(bf16[1,128,512]{2,1,0:T(8,128)(2,1)S(1)} %shard_map.145), channel_id=1, source_target_pairs={{0,4},{1,5},{2,6},{3,7},{4,0},{5,1},{6,2},{7,3},{8,12},{9,13},{10,... | collective-permute-start | bytes 393224 | tf_op jit(solution)/shard_map/ppermute | solution.py:18
  28.2 2.7 %collective-permute-start.27 = (bf16[1,128,512]{2,1,0:T(8,128)(2,1)S(1)}, bf16[1,128,512]{2,1,0:T(8,128)(2,1)S(1)}, u32[]{:S(2)}, u32[]{:S(2)}) collective-permute-start(bf16[1,128,512]{2,1,0:T(8,128)(2,1)S(1)} %shard_map.148), channel_id=1, source_target_pairs={{0,8},{1,9},{2,10},{3,11},{4,12},{5,13},{6,14},{7,15},{8,0},{9,1},... | collective-permute-start | bytes 393224 | tf_op jit(solution)/shard_map/ppermute | solution.py:18
  31.0 0.5 collective-permute-start.3
  31.5 0.6 collective-permute-start.6
  32.1 3.9 %collective-permute-done.24.refs_3_ = bf16[1,128,512]{2,1,0:T(8,128)(2,1)S(1)} collective-permute-done((bf16[1,128,512]{2,1,0:T(8,128)(2,1)S(1)}, bf16[1,128,512]{2,1,0:T(8,128)(2,1)S(1)}, u32[]{:S(2)}, u32[]{:S(2)}) %collective-permute-start.24) | collective-permute-done | bytes 131104 | tf_op jit(solution)/shard_map/ppermute | solution.py:18
  36.0 2.3 %collective-permute-done.27.refs_4_ = bf16[1,128,512]{2,1,0:T(8,128)(2,1)S(1)} collective-permute-done((bf16[1,128,512]{2,1,0:T(8,128)(2,1)S(1)}, bf16[1,128,512]{2,1,0:T(8,128)(2,1)S(1)}, u32[]{:S(2)}, u32[]{:S(2)}) %collective-permute-start.27) | collective-permute-done | bytes 131104 | tf_op jit(solution)/shard_map/ppermute | solution.py:18
  38.7 2.6 %collective-permute-start.28 = (bf16[1,128,512]{2,1,0:T(8,128)(2,1)S(1)}, bf16[1,128,512]{2,1,0:T(8,128)(2,1)S(1)}, u32[]{:S(2)}, u32[]{:S(2)}) collective-permute-start(bf16[1,128,512]{2,1,0:T(8,128)(2,1)S(1)} %get-tuple-element.33.refs_0_), channel_id=1, source_target_pairs={{0,8},{1,9},{2,10},{3,11},{4,12},{5,13},{6,14},{7,15},{8,0},{9,1},... | collective-permute-start | bytes 393224 | tf_op jit(solution)/shard_map/ppermute | solution.py:18
  41.3 1.5 %collective-permute-start.36 = (bf16[1,128,512]{2,1,0:T(8,128)(2,1)S(1)}, bf16[1,128,512]{2,1,0:T(8,128)(2,1)S(1)}, u32[]{:S(2)}, u32[]{:S(2)}) collective-permute-start(bf16[1,128,512]{2,1,0:T(8,128)(2,1)S(1)} %get-tuple-element.33.refs_0_), channel_id=1, source_target_pairs={{0,2},{1,3},{2,0},{3,1},{4,6},{5,7},{6,4},{7,5},{8,10},{9,11},{10,... | collective-permute-start | bytes 393224 | tf_op jit(solution)/shard_map/ppermute | solution.py:18
  43.3 1.7 %collective-permute-done.33.refs_2_ = bf16[1,128,512]{2,1,0:T(8,128)(2,1)S(1)} collective-permute-done((bf16[1,128,512]{2,1,0:T(8,128)(2,1)S(1)}, bf16[1,128,512]{2,1,0:T(8,128)(2,1)S(1)}, u32[]{:S(2)}, u32[]{:S(2)}) %collective-permute-start.33) | collective-permute-done | bytes 131104 | tf_op jit(solution)/shard_map/ppermute | solution.py:18
  45.0 1.0 %collective-permute-start.7 = (bf16[1,128,512]{2,1,0:T(8,128)(2,1)S(1)}, bf16[1,128,512]{2,1,0:T(8,128)(2,1)S(1)}, u32[]{:S(2)}, u32[]{:S(2)}) collective-permute-start(bf16[1,128,512]{2,1,0:T(8,128)(2,1)S(1)} %get-tuple-element.28.refs_0_), channel_id=1, source_target_pairs={{0,8},{1,9},{2,10},{3,11},{4,12},{5,13},{6,14},{7,15},{8,0},{9,1},... | collective-permute-start | bytes 393224 | tf_op jit(solution)/shard_map/ppermute | solution.py:18
  46.0 1.5 %collective-permute-start.10 = (bf16[1,128,512]{2,1,0:T(8,128)(2,1)S(1)}, bf16[1,128,512]{2,1,0:T(8,128)(2,1)S(1)}, u32[]{:S(2)}, u32[]{:S(2)}) collective-permute-start(bf16[1,128,512]{2,1,0:T(8,128)(2,1)S(1)} %get-tuple-element.28.refs_0_), channel_id=1, source_target_pairs={{0,2},{1,3},{2,0},{3,1},{4,6},{5,7},{6,4},{7,5},{8,10},{9,11},{10,... | collective-permute-start | bytes 393224 | tf_op jit(solution)/shard_map/ppermute | solution.py:18
  47.5 1.5 %collective-permute-done.28.refs_2_ = bf16[1,128,512]{2,1,0:T(8,128)(2,1)S(1)} collective-permute-done((bf16[1,128,512]{2,1,0:T(8,128)(2,1)S(1)}, bf16[1,128,512]{2,1,0:T(8,128)(2,1)S(1)}, u32[]{:S(2)}, u32[]{:S(2)}) %collective-permute-start.28) | collective-permute-done | bytes 131104 | tf_op jit(solution)/shard_map/ppermute | solution.py:18
  49.5 1.8 %collective-permute-done.16.refs_2_ = bf16[1,128,512]{2,1,0:T(8,128)(2,1)S(1)} collective-permute-done((bf16[1,128,512]{2,1,0:T(8,128)(2,1)S(1)}, bf16[1,128,512]{2,1,0:T(8,128)(2,1)S(1)}, u32[]{:S(2)}, u32[]{:S(2)}) %collective-permute-start.16) | collective-permute-done | bytes 131104 | tf_op jit(solution)/shard_map/ppermute | solution.py:18
  51.3 2.8 %collective-permute-done.7.refs_1_.refs_0_ = bf16[1,128,512]{2,1,0:T(8,128)(2,1)S(1)} collective-permute-done((bf16[1,128,512]{2,1,0:T(8,128)(2,1)S(1)}, bf16[1,128,512]{2,1,0:T(8,128)(2,1)S(1)}, u32[]{:S(2)}, u32[]{:S(2)}) %collective-permute-start.7) | collective-permute-done | bytes 131104 | tf_op jit(solution)/shard_map/ppermute | solution.py:18
  54.1 2.1 %collective-permute-start.11 = (bf16[2,128,512]{2,1,0:T(8,128)(2,1)S(1)}, bf16[2,128,512]{2,1,0:T(8,128)(2,1)S(1)}, u32[]{:S(2)}, u32[]{:S(2)}) collective-permute-start(bf16[2,128,512]{2,1,0:T(8,128)(2,1)S(1)} %shard_map.136), channel_id=1, source_target_pairs={{0,4},{1,5},{2,6},{3,7},{4,0},{5,1},{6,2},{7,3},{8,12},{9,13},{10,... | collective-permute-start | bytes 786440 | tf_op jit(solution)/shard_map/ppermute | solution.py:18
  56.2 1.5 %collective-permute-start.34 = (bf16[1,128,512]{2,1,0:T(8,128)(2,1)S(1)}, bf16[1,128,512]{2,1,0:T(8,128)(2,1)S(1)}, u32[]{:S(2)}, u32[]{:S(2)}) collective-permute-start(bf16[1,128,512]{2,1,0:T(8,128)(2,1)S(1)} %collective-permute-done.33.refs_2_), channel_id=1, source_target_pairs={{0,2},{1,3},{2,0},{3,1},{4,6},{5,7},{6,4},{7,5},{8,10},{9,11},{10,... | collective-permute-start | bytes 393224 | tf_op jit(solution)/shard_map/ppermute | solution.py:18
  58.2 2.2 %collective-permute-done.31.refs_0_ = bf16[1,128,512]{2,1,0:T(8,128)(2,1)S(1)} collective-permute-done((bf16[1,128,512]{2,1,0:T(8,128)(2,1)S(1)}, bf16[1,128,512]{2,1,0:T(8,128)(2,1)S(1)}, u32[]{:S(2)}, u32[]{:S(2)}) %collective-permute-start.31) | collective-permute-done | bytes 131104 | tf_op jit(solution)/shard_map/ppermute | solution.py:18
  60.5 2.1 %collective-permute-done.34.refs_2_ = bf16[1,128,512]{2,1,0:T(8,128)(2,1)S(1)} collective-permute-done((bf16[1,128,512]{2,1,0:T(8,128)(2,1)S(1)}, bf16[1,128,512]{2,1,0:T(8,128)(2,1)S(1)}, u32[]{:S(2)}, u32[]{:S(2)}) %collective-permute-start.34) | collective-permute-done | bytes 131104 | tf_op jit(solution)/shard_map/ppermute | solution.py:18
  62.6 1.8 %collective-permute-done.29.refs_0_ = bf16[1,128,512]{2,1,0:T(8,128)(2,1)S(1)} collective-permute-done((bf16[1,128,512]{2,1,0:T(8,128)(2,1)S(1)}, bf16[1,128,512]{2,1,0:T(8,128)(2,1)S(1)}, u32[]{:S(2)}, u32[]{:S(2)}) %collective-permute-start.29) | collective-permute-done | bytes 131104 | tf_op jit(solution)/shard_map/ppermute | solution.py:18
  64.4 1.5 %collective-permute-start.8 = (bf16[1,128,512]{2,1,0:T(8,128)(2,1)S(1)}, bf16[1,128,512]{2,1,0:T(8,128)(2,1)S(1)}, u32[]{:S(2)}, u32[]{:S(2)}) collective-permute-start(bf16[1,128,512]{2,1,0:T(8,128)(2,1)S(1)} %collective-permute-done.7.refs_1_.refs_0_), channel_id=1, source_target_pairs={{0,2},{1,3},{2,0},{3,1},{4,6},{5,7},{6,4},{7,5},{8,10},{9,11},{10,... | collective-permute-start | bytes 393224 | tf_op jit(solution)/shard_map/ppermute | solution.py:18
  65.9 2.4 %shard_map.127.tokens = bf16[1024,2048]{1,0:T(8,128)(2,1)S(1)} custom-call(bf16[1024,2048]{1,0:T(8,128)(2,1)} %tokens.1), custom_call_target="tpu_custom_call" | custom-call | flops 1000000 | bytes 1000000 | tf_op jit(solution)/shard_map/pallas_call | solution.py:30
  68.3 0.9 %shard_map.156 = (f32[128,512]{1,0:T(8,128)}, f32[128,512]{1,0:T(8,128)}) custom-call(f32[1,2]{1,0:T(1,128)S(1)} %bitcast.5, f32[128,512]{1,0:T(8,128)S(1)} %copy-done, f32[128,512]{1,0:T(8,128)S(1)} %copy-done.1, f32[128,512]{1,0:T(8,128)S(1)} %get-tuple-element.39.summed), custom_call_target="tpu_custom_call" | custom-call | flops 1000000 | bytes 1000000 | tf_op jit(solution)/shard_map/pallas_call | solution.py:30
  69.2 0.9 %shard_map.155 = (f32[128,512]{1,0:T(8,128)}, f32[128,512]{1,0:T(8,128)}) custom-call(f32[1,2]{1,0:T(1,128)S(1)} %bitcast.6, f32[128,512]{1,0:T(8,128)S(1)} %copy-done.2, f32[128,512]{1,0:T(8,128)S(1)} %copy-done.3, f32[128,512]{1,0:T(8,128)S(1)} %get-tuple-element.36.summed), custom_call_target="tpu_custom_call" | custom-call | flops 1000000 | bytes 1000000 | tf_op jit(solution)/shard_map/pallas_call | solution.py:30
  70.7 0.7 shard_map.150.refs_4_
  71.4 0.6 collective-permute-start.41
  72.3 0.7 shard_map.137.refs_4_
  73.1 0.7 shard_map.151.refs_4_
  73.9 0.6 collective-permute-start.9
  74.4 0.7 shard_map.138.refs_2_
  75.1 2.2 %collective-permute-done.41.refs_4_ = bf16[1,128,512]{2,1,0:T(8,128)(2,1)S(1)} collective-permute-done((bf16[1,128,512]{2,1,0:T(8,128)(2,1)S(1)}, bf16[1,128,512]{2,1,0:T(8,128)(2,1)S(1)}, u32[]{:S(2)}, u32[]{:S(2)}) %collective-permute-start.41) | collective-permute-done | bytes 131104 | tf_op jit(solution)/shard_map/ppermute | solution.py:18
  77.8 0.7 shard_map.152.refs_2_
  79.0 0.7 shard_map.139.refs_2_
  80.2 1.8 %shard_map.154 = (bf16[1024,512]{1,0:T(8,128)(2,1)}, bf16[1024,512]{1,0:T(8,128)(2,1)}) custom-call(bf16[1024,2048]{1,0:T(8,128)(2,1)S(1)} %shard_map.127.tokens, f32[1024,512]{1,0:T(8,128)S(1)} %shard_map.140.refs_0_, bf16[1,128,512]{2,1,0:T(8,128)(2,1)S(1)} %collective-permute-done.18.refs_1_, bf16[1,128,512]{2,1,0:T(8,128)(2,1)S(1)} %collective-permute-done.19.refs_2_, ...), custom_call_target="tpu_custom_call" | custom-call | flops 1000000 | bytes 1000000 | tf_op jit(solution)/shard_map/pallas_call | solution.py:30
  (78 shorter events, 5.2 us)
Async XLA Ops:
  2.0 5.4 %collective-permute-start.21 = (bf16[4,128,512]{2,1,0:T(8,128)(2,1)S(1)}, bf16[4,128,512]{2,1,0:T(8,128)(2,1)S(1)}, u32[]{:S(2)}, u32[]{:S(2)}) collective-permute-start(bf16[4,128,512]{2,1,0:T(8,128)(2,1)S(1)} %get-tuple-element.32), channel_id=1, source_target_pairs={{0,1},{1,0},{2,3},{3,2},{4,5},{5,4},{6,7},{7,6},{8,9},{9,8},{10,11... | collective-permute-start | bytes 1572872 | tf_op jit(solution)/shard_map/ppermute | solution.py:18
  3.9 6.6 %collective-permute-start.1 = (bf16[4,128,512]{2,1,0:T(8,128)(2,1)S(1)}, bf16[4,128,512]{2,1,0:T(8,128)(2,1)S(1)}, u32[]{:S(2)}, u32[]{:S(2)}) collective-permute-start(bf16[4,128,512]{2,1,0:T(8,128)(2,1)S(1)} %get-tuple-element.27), channel_id=1, source_target_pairs={{0,1},{1,0},{2,3},{3,2},{4,5},{5,4},{6,7},{7,6},{8,9},{9,8},{10,11... | collective-permute-start | bytes 1572872 | tf_op jit(solution)/shard_map/ppermute | solution.py:18
  5.4 7.5 %collective-permute-start.20 = (bf16[4,128,512]{2,1,0:T(8,128)(2,1)S(1)}, bf16[4,128,512]{2,1,0:T(8,128)(2,1)S(1)}, u32[]{:S(2)}, u32[]{:S(2)}) collective-permute-start(bf16[4,128,512]{2,1,0:T(8,128)(2,1)S(1)} %get-tuple-element.30), channel_id=1, source_target_pairs={{0,1},{1,0},{2,3},{3,2},{4,5},{5,4},{6,7},{7,6},{8,9},{9,8},{10,11... | collective-permute-start | bytes 1572872 | tf_op jit(solution)/shard_map/ppermute | solution.py:18
  7.3 12.6 %collective-permute-start = (bf16[4,128,512]{2,1,0:T(8,128)(2,1)S(1)}, bf16[4,128,512]{2,1,0:T(8,128)(2,1)S(1)}, u32[]{:S(2)}, u32[]{:S(2)}) collective-permute-start(bf16[4,128,512]{2,1,0:T(8,128)(2,1)S(1)} %get-tuple-element.25), channel_id=1, source_target_pairs={{0,1},{1,0},{2,3},{3,2},{4,5},{5,4},{6,7},{7,6},{8,9},{9,8},{10,11... | collective-permute-start | bytes 1572872 | tf_op jit(solution)/shard_map/ppermute | solution.py:18
  7.4 10.2 %collective-permute-start.23 = (bf16[2,128,512]{2,1,0:T(8,128)(2,1)S(1)}, bf16[2,128,512]{2,1,0:T(8,128)(2,1)S(1)}, u32[]{:S(2)}, u32[]{:S(2)}) collective-permute-start(bf16[2,128,512]{2,1,0:T(8,128)(2,1)S(1)} %shard_map.144), channel_id=1, source_target_pairs={{0,2},{1,3},{2,0},{3,1},{4,6},{5,7},{6,4},{7,5},{8,10},{9,11},{10,... | collective-permute-start | bytes 786440 | tf_op jit(solution)/shard_map/ppermute | solution.py:18
  10.5 9.3 %collective-permute-start.4 = (bf16[2,128,512]{2,1,0:T(8,128)(2,1)S(1)}, bf16[2,128,512]{2,1,0:T(8,128)(2,1)S(1)}, u32[]{:S(2)}, u32[]{:S(2)}) collective-permute-start(bf16[2,128,512]{2,1,0:T(8,128)(2,1)S(1)} %shard_map.132), channel_id=1, source_target_pairs={{0,4},{1,5},{2,6},{3,7},{4,0},{5,1},{6,2},{7,3},{8,12},{9,13},{10,... | collective-permute-start | bytes 786440 | tf_op jit(solution)/shard_map/ppermute | solution.py:18
  12.3 18.6 %collective-permute-start.2 = (bf16[2,128,512]{2,1,0:T(8,128)(2,1)S(1)}, bf16[2,128,512]{2,1,0:T(8,128)(2,1)S(1)}, u32[]{:S(2)}, u32[]{:S(2)}) collective-permute-start(bf16[2,128,512]{2,1,0:T(8,128)(2,1)S(1)} %shard_map.130), channel_id=1, source_target_pairs={{0,2},{1,3},{2,0},{3,1},{4,6},{5,7},{6,4},{7,5},{8,10},{9,11},{10,... | collective-permute-start | bytes 786440 | tf_op jit(solution)/shard_map/ppermute | solution.py:18
  12.9 13.2 %collective-permute-start.25 = (bf16[1,128,512]{2,1,0:T(8,128)(2,1)S(1)}, bf16[1,128,512]{2,1,0:T(8,128)(2,1)S(1)}, u32[]{:S(2)}, u32[]{:S(2)}) collective-permute-start(bf16[1,128,512]{2,1,0:T(8,128)(2,1)S(1)} %shard_map.146), channel_id=1, source_target_pairs={{0,2},{1,3},{2,0},{3,1},{4,6},{5,7},{6,4},{7,5},{8,10},{9,11},{10,... | collective-permute-start | bytes 393224 | tf_op jit(solution)/shard_map/ppermute | solution.py:18
  17.7 10.5 %collective-permute-start.26 = (bf16[1,128,512]{2,1,0:T(8,128)(2,1)S(1)}, bf16[1,128,512]{2,1,0:T(8,128)(2,1)S(1)}, u32[]{:S(2)}, u32[]{:S(2)}) collective-permute-start(bf16[1,128,512]{2,1,0:T(8,128)(2,1)S(1)} %shard_map.147), channel_id=1, source_target_pairs={{0,4},{1,5},{2,6},{3,7},{4,0},{5,1},{6,2},{7,3},{8,12},{9,13},{10,... | collective-permute-start | bytes 393224 | tf_op jit(solution)/shard_map/ppermute | solution.py:18
  19.9 11.6 %collective-permute-start.5 = (bf16[1,128,512]{2,1,0:T(8,128)(2,1)S(1)}, bf16[1,128,512]{2,1,0:T(8,128)(2,1)S(1)}, u32[]{:S(2)}, u32[]{:S(2)}) collective-permute-start(bf16[1,128,512]{2,1,0:T(8,128)(2,1)S(1)} %shard_map.133), channel_id=1, source_target_pairs={{0,2},{1,3},{2,0},{3,1},{4,6},{5,7},{6,4},{7,5},{8,10},{9,11},{10,... | collective-permute-start | bytes 393224 | tf_op jit(solution)/shard_map/ppermute | solution.py:18
  21.5 10.6 %collective-permute-start.22 = (bf16[1,128,512]{2,1,0:T(8,128)(2,1)S(1)}, bf16[1,128,512]{2,1,0:T(8,128)(2,1)S(1)}, u32[]{:S(2)}, u32[]{:S(2)}) collective-permute-start(bf16[1,128,512]{2,1,0:T(8,128)(2,1)S(1)} %shard_map.143), channel_id=1, source_target_pairs={{0,2},{1,3},{2,0},{3,1},{4,6},{5,7},{6,4},{7,5},{8,10},{9,11},{10,... | collective-permute-start | bytes 393224 | tf_op jit(solution)/shard_map/ppermute | solution.py:18
  22.1 16.2 %copy-start = (f32[128,512]{1,0:T(8,128)S(1)}, f32[128,512]{1,0:T(8,128)}, u32[]{:S(2)}) copy-start(f32[128,512]{1,0:T(8,128)} %master.7) | copy-start | bytes 786436
  22.2 16.2 %copy-start.1 = (f32[128,512]{1,0:T(8,128)S(1)}, f32[128,512]{1,0:T(8,128)}, u32[]{:S(2)}) copy-start(f32[128,512]{1,0:T(8,128)} %moment.7) | copy-start | bytes 786436
  22.2 16.2 %copy-start.4 = (f32[2]{0:T(128)S(1)}, f32[2]{0:T(128)}, u32[]{:S(2)}) copy-start(f32[2]{0:T(128)} %param.15) | copy-start | bytes 28
  26.1 9.9 %collective-permute-start.24 = (bf16[1,128,512]{2,1,0:T(8,128)(2,1)S(1)}, bf16[1,128,512]{2,1,0:T(8,128)(2,1)S(1)}, u32[]{:S(2)}, u32[]{:S(2)}) collective-permute-start(bf16[1,128,512]{2,1,0:T(8,128)(2,1)S(1)} %shard_map.145), channel_id=1, source_target_pairs={{0,4},{1,5},{2,6},{3,7},{4,0},{5,1},{6,2},{7,3},{8,12},{9,13},{10,... | collective-permute-start | bytes 393224 | tf_op jit(solution)/shard_map/ppermute | solution.py:18
  28.2 10.1 %collective-permute-start.27 = (bf16[1,128,512]{2,1,0:T(8,128)(2,1)S(1)}, bf16[1,128,512]{2,1,0:T(8,128)(2,1)S(1)}, u32[]{:S(2)}, u32[]{:S(2)}) collective-permute-start(bf16[1,128,512]{2,1,0:T(8,128)(2,1)S(1)} %shard_map.148), channel_id=1, source_target_pairs={{0,8},{1,9},{2,10},{3,11},{4,12},{5,13},{6,14},{7,15},{8,0},{9,1},... | collective-permute-start | bytes 393224 | tf_op jit(solution)/shard_map/ppermute | solution.py:18
  30.9 11.9 %copy-start.2 = (f32[128,512]{1,0:T(8,128)S(1)}, f32[128,512]{1,0:T(8,128)}, u32[]{:S(2)}) copy-start(f32[128,512]{1,0:T(8,128)} %master.6) | copy-start | bytes 786436
  30.9 11.9 %copy-start.3 = (f32[128,512]{1,0:T(8,128)S(1)}, f32[128,512]{1,0:T(8,128)}, u32[]{:S(2)}) copy-start(f32[128,512]{1,0:T(8,128)} %moment.6) | copy-start | bytes 786436
  31.0 10.4 %collective-permute-start.3 = (bf16[1,128,512]{2,1,0:T(8,128)(2,1)S(1)}, bf16[1,128,512]{2,1,0:T(8,128)(2,1)S(1)}, u32[]{:S(2)}, u32[]{:S(2)}) collective-permute-start(bf16[1,128,512]{2,1,0:T(8,128)(2,1)S(1)} %shard_map.131), channel_id=1, source_target_pairs={{0,4},{1,5},{2,6},{3,7},{4,0},{5,1},{6,2},{7,3},{8,12},{9,13},{10,... | collective-permute-start | bytes 393224 | tf_op jit(solution)/shard_map/ppermute | solution.py:18
  31.5 11.3 %collective-permute-start.6 = (bf16[1,128,512]{2,1,0:T(8,128)(2,1)S(1)}, bf16[1,128,512]{2,1,0:T(8,128)(2,1)S(1)}, u32[]{:S(2)}, u32[]{:S(2)}) collective-permute-start(bf16[1,128,512]{2,1,0:T(8,128)(2,1)S(1)} %shard_map.134), channel_id=1, source_target_pairs={{0,8},{1,9},{2,10},{3,11},{4,12},{5,13},{6,14},{7,15},{8,0},{9,1},... | collective-permute-start | bytes 393224 | tf_op jit(solution)/shard_map/ppermute | solution.py:18
  38.6 6.5 %collective-permute-start.33 = (bf16[1,128,512]{2,1,0:T(8,128)(2,1)S(1)}, bf16[1,128,512]{2,1,0:T(8,128)(2,1)S(1)}, u32[]{:S(2)}, u32[]{:S(2)}) collective-permute-start(bf16[1,128,512]{2,1,0:T(8,128)(2,1)S(1)} %get-tuple-element.33.refs_0_), channel_id=1, source_target_pairs={{0,4},{1,5},{2,6},{3,7},{4,0},{5,1},{6,2},{7,3},{8,12},{9,13},{10,... | collective-permute-start | bytes 393224 | tf_op jit(solution)/shard_map/ppermute | solution.py:18
  38.7 7.3 %collective-permute-start.39 = (bf16[1,128,512]{2,1,0:T(8,128)(2,1)S(1)}, bf16[1,128,512]{2,1,0:T(8,128)(2,1)S(1)}, u32[]{:S(2)}, u32[]{:S(2)}) collective-permute-start(bf16[1,128,512]{2,1,0:T(8,128)(2,1)S(1)} %get-tuple-element.33.refs_0_), channel_id=1, source_target_pairs={{0,1},{1,0},{2,3},{3,2},{4,5},{5,4},{6,7},{7,6},{8,9},{9,8},{10,11... | collective-permute-start | bytes 393224 | tf_op jit(solution)/shard_map/ppermute | solution.py:18
  38.7 10.3 %collective-permute-start.28 = (bf16[1,128,512]{2,1,0:T(8,128)(2,1)S(1)}, bf16[1,128,512]{2,1,0:T(8,128)(2,1)S(1)}, u32[]{:S(2)}, u32[]{:S(2)}) collective-permute-start(bf16[1,128,512]{2,1,0:T(8,128)(2,1)S(1)} %get-tuple-element.33.refs_0_), channel_id=1, source_target_pairs={{0,8},{1,9},{2,10},{3,11},{4,12},{5,13},{6,14},{7,15},{8,0},{9,1},... | collective-permute-start | bytes 393224 | tf_op jit(solution)/shard_map/ppermute | solution.py:18
  41.3 7.7 %collective-permute-start.36 = (bf16[1,128,512]{2,1,0:T(8,128)(2,1)S(1)}, bf16[1,128,512]{2,1,0:T(8,128)(2,1)S(1)}, u32[]{:S(2)}, u32[]{:S(2)}) collective-permute-start(bf16[1,128,512]{2,1,0:T(8,128)(2,1)S(1)} %get-tuple-element.33.refs_0_), channel_id=1, source_target_pairs={{0,2},{1,3},{2,0},{3,1},{4,6},{5,7},{6,4},{7,5},{8,10},{9,11},{10,... | collective-permute-start | bytes 393224 | tf_op jit(solution)/shard_map/ppermute | solution.py:18
  43.1 8.2 %collective-permute-start.16 = (bf16[1,128,512]{2,1,0:T(8,128)(2,1)S(1)}, bf16[1,128,512]{2,1,0:T(8,128)(2,1)S(1)}, u32[]{:S(2)}, u32[]{:S(2)}) collective-permute-start(bf16[1,128,512]{2,1,0:T(8,128)(2,1)S(1)} %get-tuple-element.28.refs_0_), channel_id=1, source_target_pairs={{0,4},{1,5},{2,6},{3,7},{4,0},{5,1},{6,2},{7,3},{8,12},{9,13},{10,... | collective-permute-start | bytes 393224 | tf_op jit(solution)/shard_map/ppermute | solution.py:18
  45.0 9.0 %collective-permute-start.7 = (bf16[1,128,512]{2,1,0:T(8,128)(2,1)S(1)}, bf16[1,128,512]{2,1,0:T(8,128)(2,1)S(1)}, u32[]{:S(2)}, u32[]{:S(2)}) collective-permute-start(bf16[1,128,512]{2,1,0:T(8,128)(2,1)S(1)} %get-tuple-element.28.refs_0_), channel_id=1, source_target_pairs={{0,8},{1,9},{2,10},{3,11},{4,12},{5,13},{6,14},{7,15},{8,0},{9,1},... | collective-permute-start | bytes 393224 | tf_op jit(solution)/shard_map/ppermute | solution.py:18
  46.0 8.1 %collective-permute-start.10 = (bf16[1,128,512]{2,1,0:T(8,128)(2,1)S(1)}, bf16[1,128,512]{2,1,0:T(8,128)(2,1)S(1)}, u32[]{:S(2)}, u32[]{:S(2)}) collective-permute-start(bf16[1,128,512]{2,1,0:T(8,128)(2,1)S(1)} %get-tuple-element.28.refs_0_), channel_id=1, source_target_pairs={{0,2},{1,3},{2,0},{3,1},{4,6},{5,7},{6,4},{7,5},{8,10},{9,11},{10,... | collective-permute-start | bytes 393224 | tf_op jit(solution)/shard_map/ppermute | solution.py:18
  49.0 5.1 %collective-permute-start.15 = (bf16[1,128,512]{2,1,0:T(8,128)(2,1)S(1)}, bf16[1,128,512]{2,1,0:T(8,128)(2,1)S(1)}, u32[]{:S(2)}, u32[]{:S(2)}) collective-permute-start(bf16[1,128,512]{2,1,0:T(8,128)(2,1)S(1)} %get-tuple-element.28.refs_0_), channel_id=1, source_target_pairs={{0,1},{1,0},{2,3},{3,2},{4,5},{5,4},{6,7},{7,6},{8,9},{9,8},{10,11... | collective-permute-start | bytes 393224 | tf_op jit(solution)/shard_map/ppermute | solution.py:18
  49.0 7.2 %collective-permute-start.40 = (bf16[1,128,512]{2,1,0:T(8,128)(2,1)S(1)}, bf16[1,128,512]{2,1,0:T(8,128)(2,1)S(1)}, u32[]{:S(2)}, u32[]{:S(2)}) collective-permute-start(bf16[1,128,512]{2,1,0:T(8,128)(2,1)S(1)} %collective-permute-done.33.refs_2_), channel_id=1, source_target_pairs={{0,1},{1,0},{2,3},{3,2},{4,5},{5,4},{6,7},{7,6},{8,9},{9,8},{10,11... | collective-permute-start | bytes 393224 | tf_op jit(solution)/shard_map/ppermute | solution.py:18
  51.3 6.4 %collective-permute-start.38 = (bf16[1,128,512]{2,1,0:T(8,128)(2,1)S(1)}, bf16[1,128,512]{2,1,0:T(8,128)(2,1)S(1)}, u32[]{:S(2)}, u32[]{:S(2)}) collective-permute-start(bf16[1,128,512]{2,1,0:T(8,128)(2,1)S(1)} %collective-permute-done.28.refs_2_), channel_id=1, source_target_pairs={{0,1},{1,0},{2,3},{3,2},{4,5},{5,4},{6,7},{7,6},{8,9},{9,8},{10,11... | collective-permute-start | bytes 393224 | tf_op jit(solution)/shard_map/ppermute | solution.py:18
  54.1 4.2 %collective-permute-start.37 = (bf16[1,128,512]{2,1,0:T(8,128)(2,1)S(1)}, bf16[1,128,512]{2,1,0:T(8,128)(2,1)S(1)}, u32[]{:S(2)}, u32[]{:S(2)}) collective-permute-start(bf16[1,128,512]{2,1,0:T(8,128)(2,1)S(1)} %collective-permute-done.36.refs_0_), channel_id=1, source_target_pairs={{0,1},{1,0},{2,3},{3,2},{4,5},{5,4},{6,7},{7,6},{8,9},{9,8},{10,11... | collective-permute-start | bytes 393224 | tf_op jit(solution)/shard_map/ppermute | solution.py:18
  54.1 6.4 %collective-permute-start.31 = (bf16[1,128,512]{2,1,0:T(8,128)(2,1)S(1)}, bf16[1,128,512]{2,1,0:T(8,128)(2,1)S(1)}, u32[]{:S(2)}, u32[]{:S(2)}) collective-permute-start(bf16[1,128,512]{2,1,0:T(8,128)(2,1)S(1)} %collective-permute-done.28.refs_2_), channel_id=1, source_target_pairs={{0,4},{1,5},{2,6},{3,7},{4,0},{5,1},{6,2},{7,3},{8,12},{9,13},{10,... | collective-permute-start | bytes 393224 | tf_op jit(solution)/shard_map/ppermute | solution.py:18
  54.1 16.5 %collective-permute-start.11 = (bf16[2,128,512]{2,1,0:T(8,128)(2,1)S(1)}, bf16[2,128,512]{2,1,0:T(8,128)(2,1)S(1)}, u32[]{:S(2)}, u32[]{:S(2)}) collective-permute-start(bf16[2,128,512]{2,1,0:T(8,128)(2,1)S(1)} %shard_map.136), channel_id=1, source_target_pairs={{0,4},{1,5},{2,6},{3,7},{4,0},{5,1},{6,2},{7,3},{8,12},{9,13},{10,... | collective-permute-start | bytes 786440 | tf_op jit(solution)/shard_map/ppermute | solution.py:18
  56.2 6.4 %collective-permute-start.34 = (bf16[1,128,512]{2,1,0:T(8,128)(2,1)S(1)}, bf16[1,128,512]{2,1,0:T(8,128)(2,1)S(1)}, u32[]{:S(2)}, u32[]{:S(2)}) collective-permute-start(bf16[1,128,512]{2,1,0:T(8,128)(2,1)S(1)} %collective-permute-done.33.refs_2_), channel_id=1, source_target_pairs={{0,2},{1,3},{2,0},{3,1},{4,6},{5,7},{6,4},{7,5},{8,10},{9,11},{10,... | collective-permute-start | bytes 393224 | tf_op jit(solution)/shard_map/ppermute | solution.py:18
  57.7 6.6 %collective-permute-start.29 = (bf16[1,128,512]{2,1,0:T(8,128)(2,1)S(1)}, bf16[1,128,512]{2,1,0:T(8,128)(2,1)S(1)}, u32[]{:S(2)}, u32[]{:S(2)}) collective-permute-start(bf16[1,128,512]{2,1,0:T(8,128)(2,1)S(1)} %collective-permute-done.28.refs_2_), channel_id=1, source_target_pairs={{0,2},{1,3},{2,0},{3,1},{4,6},{5,7},{6,4},{7,5},{8,10},{9,11},{10,... | collective-permute-start | bytes 393224 | tf_op jit(solution)/shard_map/ppermute | solution.py:18
  58.2 7.6 %collective-permute-start.17 = (bf16[1,128,512]{2,1,0:T(8,128)(2,1)S(1)}, bf16[1,128,512]{2,1,0:T(8,128)(2,1)S(1)}, u32[]{:S(2)}, u32[]{:S(2)}) collective-permute-start(bf16[1,128,512]{2,1,0:T(8,128)(2,1)S(1)} %collective-permute-done.16.refs_2_), channel_id=1, source_target_pairs={{0,1},{1,0},{2,3},{3,2},{4,5},{5,4},{6,7},{7,6},{8,9},{9,8},{10,11... | collective-permute-start | bytes 393224 | tf_op jit(solution)/shard_map/ppermute | solution.py:18
  60.5 9.6 %collective-permute-start.13 = (bf16[1,128,512]{2,1,0:T(8,128)(2,1)S(1)}, bf16[1,128,512]{2,1,0:T(8,128)(2,1)S(1)}, u32[]{:S(2)}, u32[]{:S(2)}) collective-permute-start(bf16[1,128,512]{2,1,0:T(8,128)(2,1)S(1)} %collective-permute-done.7.refs_1_.refs_0_), channel_id=1, source_target_pairs={{0,1},{1,0},{2,3},{3,2},{4,5},{5,4},{6,7},{7,6},{8,9},{9,8},{10,11... | collective-permute-start | bytes 393224 | tf_op jit(solution)/shard_map/ppermute | solution.py:18
  62.6 8.8 %collective-permute-start.14 = (bf16[1,128,512]{2,1,0:T(8,128)(2,1)S(1)}, bf16[1,128,512]{2,1,0:T(8,128)(2,1)S(1)}, u32[]{:S(2)}, u32[]{:S(2)}) collective-permute-start(bf16[1,128,512]{2,1,0:T(8,128)(2,1)S(1)} %collective-permute-done.10.refs_0_.refs_2_), channel_id=1, source_target_pairs={{0,1},{1,0},{2,3},{3,2},{4,5},{5,4},{6,7},{7,6},{8,9},{9,8},{10,11... | collective-permute-start | bytes 393224 | tf_op jit(solution)/shard_map/ppermute | solution.py:18
  64.4 7.6 %collective-permute-start.8 = (bf16[1,128,512]{2,1,0:T(8,128)(2,1)S(1)}, bf16[1,128,512]{2,1,0:T(8,128)(2,1)S(1)}, u32[]{:S(2)}, u32[]{:S(2)}) collective-permute-start(bf16[1,128,512]{2,1,0:T(8,128)(2,1)S(1)} %collective-permute-done.7.refs_1_.refs_0_), channel_id=1, source_target_pairs={{0,2},{1,3},{2,0},{3,1},{4,6},{5,7},{6,4},{7,5},{8,10},{9,11},{10,... | collective-permute-start | bytes 393224 | tf_op jit(solution)/shard_map/ppermute | solution.py:18
  65.9 7.2 %collective-permute-start.32 = (bf16[1,128,512]{2,1,0:T(8,128)(2,1)S(1)}, bf16[1,128,512]{2,1,0:T(8,128)(2,1)S(1)}, u32[]{:S(2)}, u32[]{:S(2)}) collective-permute-start(bf16[1,128,512]{2,1,0:T(8,128)(2,1)S(1)} %collective-permute-done.31.refs_0_), channel_id=1, source_target_pairs={{0,1},{1,0},{2,3},{3,2},{4,5},{5,4},{6,7},{7,6},{8,9},{9,8},{10,11... | collective-permute-start | bytes 393224 | tf_op jit(solution)/shard_map/ppermute | solution.py:18
  70.1 3.8 %collective-permute-start.35 = (bf16[1,128,512]{2,1,0:T(8,128)(2,1)S(1)}, bf16[1,128,512]{2,1,0:T(8,128)(2,1)S(1)}, u32[]{:S(2)}, u32[]{:S(2)}) collective-permute-start(bf16[1,128,512]{2,1,0:T(8,128)(2,1)S(1)} %collective-permute-done.34.refs_2_), channel_id=1, source_target_pairs={{0,1},{1,0},{2,3},{3,2},{4,5},{5,4},{6,7},{7,6},{8,9},{9,8},{10,11... | collective-permute-start | bytes 393224 | tf_op jit(solution)/shard_map/ppermute | solution.py:18
  70.6 8.4 %collective-permute-start.12 = (bf16[2,128,512]{2,1,0:T(8,128)(2,1)S(1)}, bf16[2,128,512]{2,1,0:T(8,128)(2,1)S(1)}, u32[]{:S(2)}, u32[]{:S(2)}) collective-permute-start(bf16[2,128,512]{2,1,0:T(8,128)(2,1)S(1)} %collective-permute-done.11.refs_0_), channel_id=1, source_target_pairs={{0,1},{1,0},{2,3},{3,2},{4,5},{5,4},{6,7},{7,6},{8,9},{9,8},{10,11... | collective-permute-start | bytes 786440 | tf_op jit(solution)/shard_map/ppermute | solution.py:18
  71.4 5.9 %collective-permute-start.41 = (bf16[1,128,512]{2,1,0:T(8,128)(2,1)S(1)}, bf16[1,128,512]{2,1,0:T(8,128)(2,1)S(1)}, u32[]{:S(2)}, u32[]{:S(2)}) collective-permute-start(bf16[1,128,512]{2,1,0:T(8,128)(2,1)S(1)} %collective-permute-done.31.refs_0_), channel_id=1, source_target_pairs={{0,2},{1,3},{2,0},{3,1},{4,6},{5,7},{6,4},{7,5},{8,10},{9,11},{10,... | collective-permute-start | bytes 393224 | tf_op jit(solution)/shard_map/ppermute | solution.py:18
  72.0 5.6 %collective-permute-start.18 = (bf16[1,128,512]{2,1,0:T(8,128)(2,1)S(1)}, bf16[1,128,512]{2,1,0:T(8,128)(2,1)S(1)}, u32[]{:S(2)}, u32[]{:S(2)}) collective-permute-start(bf16[1,128,512]{2,1,0:T(8,128)(2,1)S(1)} %collective-permute-done.8.refs_0_), channel_id=1, source_target_pairs={{0,4},{1,5},{2,6},{3,7},{4,0},{5,1},{6,2},{7,3},{8,12},{9,13},{10,... | collective-permute-start | bytes 393224 | tf_op jit(solution)/shard_map/ppermute | solution.py:18
  73.1 5.5 %collective-permute-start.30 = (bf16[1,128,512]{2,1,0:T(8,128)(2,1)S(1)}, bf16[1,128,512]{2,1,0:T(8,128)(2,1)S(1)}, u32[]{:S(2)}, u32[]{:S(2)}) collective-permute-start(bf16[1,128,512]{2,1,0:T(8,128)(2,1)S(1)} %collective-permute-done.29.refs_0_), channel_id=1, source_target_pairs={{0,1},{1,0},{2,3},{3,2},{4,5},{5,4},{6,7},{7,6},{8,9},{9,8},{10,11... | collective-permute-start | bytes 393224 | tf_op jit(solution)/shard_map/ppermute | solution.py:18
  73.9 5.8 %collective-permute-start.9 = (bf16[1,128,512]{2,1,0:T(8,128)(2,1)S(1)}, bf16[1,128,512]{2,1,0:T(8,128)(2,1)S(1)}, u32[]{:S(2)}, u32[]{:S(2)}) collective-permute-start(bf16[1,128,512]{2,1,0:T(8,128)(2,1)S(1)} %collective-permute-done.8.refs_0_), channel_id=1, source_target_pairs={{0,1},{1,0},{2,3},{3,2},{4,5},{5,4},{6,7},{7,6},{8,9},{9,8},{10,11... | collective-permute-start | bytes 393224 | tf_op jit(solution)/shard_map/ppermute | solution.py:18
  77.3 2.9 %collective-permute-start.42 = (bf16[1,128,512]{2,1,0:T(8,128)(2,1)S(1)}, bf16[1,128,512]{2,1,0:T(8,128)(2,1)S(1)}, u32[]{:S(2)}, u32[]{:S(2)}) collective-permute-start(bf16[1,128,512]{2,1,0:T(8,128)(2,1)S(1)} %collective-permute-done.41.refs_4_), channel_id=1, source_target_pairs={{0,1},{1,0},{2,3},{3,2},{4,5},{5,4},{6,7},{7,6},{8,9},{9,8},{10,11... | collective-permute-start | bytes 393224 | tf_op jit(solution)/shard_map/ppermute | solution.py:18
  77.5 2.6 %collective-permute-start.19 = (bf16[1,128,512]{2,1,0:T(8,128)(2,1)S(1)}, bf16[1,128,512]{2,1,0:T(8,128)(2,1)S(1)}, u32[]{:S(2)}, u32[]{:S(2)}) collective-permute-start(bf16[1,128,512]{2,1,0:T(8,128)(2,1)S(1)} %collective-permute-done.18.refs_1_), channel_id=1, source_target_pairs={{0,1},{1,0},{2,3},{3,2},{4,5},{5,4},{6,7},{7,6},{8,9},{9,8},{10,11... | collective-permute-start | bytes 393224 | tf_op jit(solution)/shard_map/ppermute | solution.py:18
